TPU v7x, 512 devices: a whole 4x4x16 slice. The times are simulated.
512 devices in a mesh: row: 32 (over x_lo, z), col: 16 (over y, x_hi, core).
Axes of the slice: x: 4 (x_hi: 2, x_lo: 2; x = x_hi * 2 + x_lo), y: 4, z: 16, core: 2. Of those that a mesh axis runs over, the one named last changes fastest.
Arguments:
- gradient: bfloat16 [8192, 28672], P('row', 'col'), may hold values from -6 to 6
- projector: bfloat16 [8192, 1024], P('row'), may hold values from -0.375 to 0.375
- first_moment: float32 [1024, 28672], P('row', 'col'), may hold values from -6 to 6
- second_moment: float32 [1024, 28672], P('row', 'col'), may hold values from 5e-05 to 0.12, as said below
Outputs:
- update: bfloat16 [8192, 28672], P('row', 'col')
- first_new: float32 [1024, 28672], P('row', 'col')
- second_new: float32 [1024, 28672], P('row', 'col')
Inputs may be any that keep to these rules, and one draw needn't show every extreme that they name: `second_moment`: entries are positive.
All inputs are finite; a program needn't handle non-finite values.
Results may differ from a plain program's by a relative error of at most 0.038.
Values may be sent and summed in bfloat16 or wider, within the bound.
No kernel may reach another device: no remote copies, remote signals or barrier semaphores. Data moves between devices by JAX's collectives and lax.ppermute only.
A program may use at most 64 MiB of HBM per device.

v0:
```python
import functools

import jax
import jax.numpy as jnp
from jax import lax
from jax.sharding import Mesh
from jax.sharding import PartitionSpec as P

FF = 28672
R = 1024
ROW = ("row_0", "row_1")
ROW_COL = ("row_0", "row_1", "col_0", "col_1", "col_2")
COL = ("col_0", "col_1", "col_2")


decay_first = 0.9
decay_second = 0.999
bias_first = 1.0 - 0.9**10
bias_second = 1.0 - 0.999**10
epsilon = 1e-08
clip_limit = 0.5


def sum_in_order(pieces, axes, order):
    lengths = [lax.axis_size(a) for a in axes]
    pieces = pieces.reshape(*lengths, *pieces.shape[1:])
    pieces = pieces.transpose(*order, *range(len(axes), pieces.ndim))
    pieces = pieces.reshape(-1, *pieces.shape[len(axes) :])
    for k in order:
        pieces = lax.psum_scatter(pieces, axes[k], scatter_dimension=0, tiled=True)
    return pieces[0]


def in_blocks(shard, dim, length):
    before, after = (shard.shape[:dim], shard.shape[dim + 1 :])
    return jnp.moveaxis(shard.reshape(*before, length, -1, *after), dim, 0)


def summed_rows(shard, axes, order, dim):
    length = lax.axis_size(axes)
    return sum_in_order(in_blocks(shard, dim, length), axes, order)


def by_axis(shard, axes):
    return functools.reduce(lax.psum, axes, shard)


def laid_out(pieces, dim):
    pieces = jnp.moveaxis(pieces, 0, dim)
    lengths = pieces.shape
    return pieces.reshape(*lengths[:dim], lengths[dim] * lengths[dim + 1], *lengths[dim + 2 :])


def all_blocks(shard, axes, order):
    pieces = shard[None]
    for k in order:
        pieces = lax.all_gather(pieces, axes[k], axis=0, tiled=True)
    carried = [lax.axis_size(axes[k]) for k in reversed(order)]
    pieces = pieces.reshape(*carried, *shard.shape)
    turned = sorted(range(len(order)), key=lambda place: order[len(order) - 1 - place])
    return pieces.transpose(*turned, *range(len(order), pieces.ndim)).reshape(-1, *shard.shape)


def gathered_by_axis(shard, axes, order, dim):
    return laid_out(all_blocks(shard, axes, order), dim)


def local(gradient, projector, first_moment, second_moment):
    chosen = projector
    product = lax.dot_general(
        chosen, gradient, (((0,), (0,)), ((), ())), preferred_element_type=jnp.float32
    )
    rounded = lax.optimization_barrier(product.astype(jnp.bfloat16))
    lowrank = summed_rows(rounded.astype(jnp.float32).astype(jnp.bfloat16), ROW, (1, 0), 0).astype(
        jnp.float32
    )
    first_new = decay_first * first_moment + (1.0 - decay_first) * lowrank
    second_new = decay_second * second_moment + (1.0 - decay_second) * lowrank * lowrank
    direction = first_new / bias_first / (jnp.sqrt(second_new / bias_second) + epsilon)
    square_total = jnp.sum(direction * direction)
    total = by_axis(square_total, ROW_COL)
    root_mean = jnp.sqrt(total / (R * FF) + 1e-06)
    factor = jnp.minimum(1.0, clip_limit / root_mean)
    step_low = (factor * direction).astype(jnp.bfloat16)
    chosen = projector
    projected = jnp.dot(
        chosen, gathered_by_axis(step_low, ROW, (0, 1), 0), preferred_element_type=jnp.float32
    )
    updates = projected.astype(jnp.bfloat16)
    return (updates, first_new, second_new)


def solution(mesh):
    torus = Mesh(
        mesh.devices.reshape(2, 16, 4, 2, 2), ("row_0", "row_1", "col_0", "col_1", "col_2")
    )
    in_specs = (P(ROW, COL), P(ROW, None), P(ROW, COL), P(ROW, COL))
    out_specs = (P(ROW, COL), P(ROW, COL), P(ROW, COL))
    return jax.shard_map(local, mesh=torus, in_specs=in_specs, out_specs=out_specs, check_vma=False)
```

profile of v0, /device:TPU:2, one launch (start us, length us, event | category | flops | bytes accessed | tf_op | source)
XLA Modules:
  0.0 269.5 jit_solution(13238906403567828522)
XLA Ops:
  7.2 0.0 copy-start
  7.2 0.0 reduce-scatter.3.cloned.1.call-start
  7.2 1.1 copy-done
  8.3 2.2 convolution_convert_fusion
  10.6 2.1 copy.14
  12.7 0.0 reduce-scatter.3.cloned.1.call-update
  12.7 0.0 reduce-scatter.5.cloned.1.call-start
  12.7 83.8 %reduce-scatter.3.cloned.1.call-done = bf16[2,32,1792]{2,1,0:T(8,128)(2,1)} async-done(((bf16[32,32,1792]{2,1,0:T(8,128)(2,1)}), bf16[2,32,1792]{2,1,0:T(8,128)(2,1)}) %reduce-scatter.3.cloned.1.call-update) | async-done | bytes 229392 | tf_op jit(solution)/shard_map/reduce_scatter | solution.py:30
  96.6 0.0 reduce-scatter.5.cloned.1.call-update
  96.6 0.0 all-gather.3.cloned.1.call-start
  96.6 21.2 %reduce-scatter.5.cloned.1.call-done = bf16[1,32,1792]{2,1,0:T(8,128)(2,1)} async-done(((bf16[2,32,1792]{2,1,0:T(8,128)(2,1)}), bf16[1,32,1792]{2,1,0:T(8,128)(2,1)}) %reduce-scatter.5.cloned.1.call-update) | async-done | bytes 114704 | tf_op jit(solution)/shard_map/reduce_scatter | solution.py:30
  117.8 1.7 multiply_reduce_fusion
  119.5 5.5 %psum.35 = f32[]{:T(128)} all-reduce(f32[]{:T(128)} %get-tuple-element.15), channel_id=1, replica_groups=mesh['row_0'=2,'row_1'=16,'col_0'=4,'col_1'=2,'col_2'=2] {'row_0'}, use_global_device_ids=true, to_apply=%region_3.0 | all-reduce | flops 1 | bytes 8 | tf_op jit(solution)/shard_map/psum | solution.py:45
  125.0 31.7 %psum.36 = f32[]{:T(128)} all-reduce(f32[]{:T(128)} %psum.35), channel_id=1, replica_groups=mesh['row_0'=2,'row_1'=16,'col_0'=4,'col_1'=2,'col_2'=2] {'row_1'}, use_global_device_ids=true, to_apply=%region_4.0 | all-reduce | flops 1 | bytes 8 | tf_op jit(solution)/shard_map/psum | solution.py:45
  156.7 11.1 %psum.37 = f32[]{:T(128)} all-reduce(f32[]{:T(128)} %psum.36), channel_id=1, replica_groups=mesh['row_0'=2,'row_1'=16,'col_0'=4,'col_1'=2,'col_2'=2] {'col_0'}, use_global_device_ids=true, to_apply=%region_5.0 | all-reduce | flops 1 | bytes 8 | tf_op jit(solution)/shard_map/psum | solution.py:45
  167.8 7.0 %psum.38 = f32[]{:T(128)} all-reduce(f32[]{:T(128)} %psum.37), channel_id=1, replica_groups=mesh['row_0'=2,'row_1'=16,'col_0'=4,'col_1'=2,'col_2'=2] {'col_1'}, use_global_device_ids=true, to_apply=%region_6.0 | all-reduce | flops 1 | bytes 8 | tf_op jit(solution)/shard_map/psum | solution.py:45
  174.9 3.1 %psum.39 = f32[]{:T(128)} all-reduce(f32[]{:T(128)} %psum.38), channel_id=1, replica_groups=mesh['row_0'=2,'row_1'=16,'col_0'=4,'col_1'=2,'col_2'=2] {'col_2'}, use_global_device_ids=true, to_apply=%region_7.0 | all-reduce | flops 1 | bytes 8 | tf_op jit(solution)/shard_map/psum | solution.py:45
  178.6 0.1 multiply_convert_fusion
  178.8 6.0 %all-gather = bf16[64,1792]{1,0:T(8,128)(2,1)} all-gather(bf16[32,1792]{1,0:T(8,128)(2,1)S(1)} %multiply_convert_fusion), channel_id=2, replica_groups=mesh['row_0'=2,'row_1'=16,'col_0'=4,'col_1'=2,'col_2'=2] {'row_0'}, dimensions={0}, use_global_device_ids=true | all-gather | bytes 344064 | tf_op jit(solution)/shard_map/all_gather | solution.py:57
  184.7 0.0 all-gather.3.cloned.1.call-update
  184.8 73.3 %all-gather.3.cloned.1.call-done = bf16[32,32,1792]{2,1,0:T(8,128)(2,1)} async-done(((bf16[2,32,1792]{2,1,0:T(8,128)(2,1)}), bf16[32,32,1792]{2,1,0:T(8,128)(2,1)}) %all-gather.3.cloned.1.call-update) | async-done | bytes 3670032 | tf_op jit(solution)/shard_map/all_gather | solution.py:57
  258.1 2.4 copy.15
  260.4 1.2 fusion
  261.6 1.4 copy.16
  (10 shorter events, 0.0 us)
Async XLA Ops:
  7.2 1.2 copy-start
  7.2 89.4 %reduce-scatter.3.cloned.1.call-start = ((), (), s32[]{:S(2)}) async-start(), calls=%async_computation.2 | async-start | bytes 3899392 | tf_op jit(solution)/shard_map/reduce_scatter | solution.py:30
  12.7 105.1 %copy-start.4 = (f32[32,1792]{1,0:T(8,128)S(1)}, f32[32,1792]{1,0:T(8,128)}, u32[]{:S(2)}) copy-start(f32[32,1792]{1,0:T(8,128)} %param.6) | copy-start | bytes 688132
  12.7 105.1 %copy-start.5 = (f32[32,1792]{1,0:T(8,128)S(1)}, f32[32,1792]{1,0:T(8,128)}, u32[]{:S(2)}) copy-start(f32[32,1792]{1,0:T(8,128)} %param.7) | copy-start | bytes 688132
  12.7 105.1 %reduce-scatter.5.cloned.1.call-start = ((), (), s32[]{:S(2)}) async-start(), calls=%async_computation.3 | async-start | bytes 344064 | tf_op jit(solution)/shard_map/reduce_scatter | solution.py:30
  96.6 161.5 %all-gather.3.cloned.1.call-start = ((), (), s32[]{:S(2)}) async-start(), calls=%async_computation.4 | async-start | bytes 3899392 | tf_op jit(solution)/shard_map/all_gather | solution.py:57
  119.5 140.9 %copy-start.2 = (f32[32,1792]{1,0:T(8,128)}, f32[32,1792]{1,0:T(8,128)S(1)}, u32[]{:S(2)}) copy-start(f32[32,1792]{1,0:T(8,128)S(1)} %get-tuple-element.16) | copy-start | bytes 688132
  119.5 140.9 %copy-start.3 = (f32[32,1792]{1,0:T(8,128)}, f32[32,1792]{1,0:T(8,128)S(1)}, u32[]{:S(2)}) copy-start(f32[32,1792]{1,0:T(8,128)S(1)} %get-tuple-element.17) | copy-start | bytes 688132
  258.1 2.4 copy-start.1
Sparse Core Ops, SparseCore 0:
  12.8 83.7 reduce-scatter.2
  99.4 18.3 reduce-scatter.4
  184.9 73.1 all-gather.2
where the time goes:
time: 270 us
  waiting for transfers between devices  178 us (66%)
  blocking collectives  64.4 us (24%)
  between operations  14.5 us (5%)
  local copies, waits for them, and re-layouts  6.97 us (3%)
  matrix products  3.39 us (1%)
    reduce_scatter x2, waiting for transfers between devices, sum_in_order(): pieces = lax.psum_scatter(pieces, axes[k], scatter_dimension=0, tiled=True)  105 us
    all_gather x1, waiting for transfers between devices, all_blocks(): pieces = lax.all_gather(pieces, axes[k], axis=0, tiled=True)  73.3 us
    psum x5, blocking collectives, by_axis(): return functools.reduce(lax.psum, axes, shard)  58.5 us
    all_gather x1, blocking collectives, all_blocks(): pieces = lax.all_gather(pieces, axes[k], axis=0, tiled=True)  5.99 us
  transfers between devices with their start and end apart: 3, of which 3 were waited for; matrix products, arithmetic and copies ran while one was open for 0% of the time, Pallas kernels for 0%

commit v1 on v0

v1 whole, which is shorter than its diff:
```python
import functools

import jax
import jax.numpy as jnp
from jax import lax
from jax.sharding import Mesh
from jax.sharding import PartitionSpec as P

FF = 28672
R = 1024
ROW = ("row_0", "row_1")
ROW_COL = ("row_0", "row_1", "col_0", "col_1", "col_2")
COL = ("col_0", "col_1", "col_2")


decay_first = 0.9
decay_second = 0.999
bias_first = 1.0 - 0.9**10
bias_second = 1.0 - 0.999**10
epsilon = 1e-08
clip_limit = 0.5


def by_axis(shard, axes):
    return functools.reduce(lax.psum, axes, shard)


def exchanged(pieces, axis):
    return lax.all_to_all(pieces, axis, split_axis=0, concat_axis=0, tiled=True)


def local(gradient, projector, first_moment, second_moment):
    row_0, row_1 = (lax.axis_size(a) for a in ROW)
    rows = first_moment.shape[0]
    product = lax.dot_general(
        projector, gradient, (((0,), (0,)), ((), ())), preferred_element_type=jnp.float32
    )
    pieces = product.astype(jnp.bfloat16).reshape(row_0, row_1, rows, -1).swapaxes(0, 1)
    pieces = lax.psum_scatter(
        pieces.reshape(row_1 * row_0, rows, -1), "row_1", scatter_dimension=0, tiled=True
    )
    pair = exchanged(pieces, "row_0").astype(jnp.float32)
    lowrank = pair[0] + pair[1]
    first_new = decay_first * first_moment + (1.0 - decay_first) * lowrank
    second_new = decay_second * second_moment + (1.0 - decay_second) * lowrank * lowrank
    direction = first_new / bias_first / (jnp.sqrt(second_new / bias_second) + epsilon)
    gathered = direction.astype(jnp.bfloat16)[None]
    for axis in ("row_0", "row_1"):
        gathered = lax.all_gather(gathered, axis, axis=0, tiled=True)
    total = by_axis(jnp.sum(direction * direction), ROW_COL)
    root_mean = jnp.sqrt(total / (R * FF) + 1e-06)
    factor = jnp.minimum(1.0, clip_limit / root_mean)
    basis = projector.reshape(-1, row_0, row_1, rows).swapaxes(1, 2).reshape(projector.shape)
    basis = lax.optimization_barrier(basis)
    projected = jnp.dot(
        basis, gathered.reshape(basis.shape[1], -1), preferred_element_type=jnp.float32
    )
    updates = (factor * projected).astype(jnp.bfloat16)
    return (updates, first_new, second_new)


def solution(mesh):
    torus = Mesh(
        mesh.devices.reshape(2, 16, 4, 2, 2), ("row_0", "row_1", "col_0", "col_1", "col_2")
    )
    in_specs = (P(ROW, COL), P(ROW, None), P(ROW, COL), P(ROW, COL))
    out_specs = (P(ROW, COL), P(ROW, COL), P(ROW, COL))
    return jax.shard_map(local, mesh=torus, in_specs=in_specs, out_specs=out_specs, check_vma=False)
```

time: 270 us -> 198 us (0.73)
  waiting for transfers between devices: 178 us -> 103 us
  blocking collectives: 64.4 us -> 68.2 us
    all_gather x1, waiting for transfers between devices: 73.3 us -> 19.5 us  [local(): gathered = lax.all_gather(gathered, axis, axis=0, tiled=True)]
    reduce_scatter x2 -> x1, waiting for transfers between devices: 105 us -> 83.8 us  [local(): lax.psum_scatter(pieces.reshape(row_1 * row_0, rows, -1), 'row_1', scatte...]
    all_to_all x0 -> x1, blocking collectives: none -> 6.99 us  [exchanged(): return lax.all_to_all(pieces, axis, split_axis=0, concat_axis=0, tiled=True)]
    psum x5, blocking collectives: 58.5 us -> 55.6 us  [by_axis(): return functools.reduce(lax.psum, axes, shard)]
  transfers between devices with their start and end apart: 3 -> 2, of which waited for: 3 -> 2; matrix products, arithmetic and copies ran while one was open for 0% -> 0% of each run, Pallas kernels for 0% -> 0%
where the time goes in v1:
time: 198 us
  waiting for transfers between devices  103 us (52%)
  blocking collectives  68.2 us (34%)
  between operations  14.8 us (7%)
  matrix products  5.41 us (3%)
  local copies, waits for them, and re-layouts  4.85 us (2%)
    reduce_scatter x1, waiting for transfers between devices, local(): lax.psum_scatter(pieces.reshape(row_1 * row_0, rows, -1), 'row_1', scatte...  83.8 us
    psum x5, blocking collectives, by_axis(): return functools.reduce(lax.psum, axes, shard)  55.6 us
    all_gather x1, waiting for transfers between devices, local(): gathered = lax.all_gather(gathered, axis, axis=0, tiled=True)  19.5 us
    all_to_all x1, blocking collectives, exchanged(): return lax.all_to_all(pieces, axis, split_axis=0, concat_axis=0, tiled=True)  6.99 us
    all_gather x1, blocking collectives, local(): gathered = lax.all_gather(gathered, axis, axis=0, tiled=True)  5.57 us
  transfers between devices with their start and end apart: 2, of which 2 were waited for; matrix products, arithmetic and copies ran while one was open for 0% of the time, Pallas kernels for 0%

profile of v1, /device:TPU:2, one launch (start us, length us, event | category | flops | bytes accessed | tf_op | source)
XLA Modules:
  0.0 197.7 jit_solution(11366122901865304837)
XLA Ops:
  7.2 0.0 copy-start
  7.2 0.0 reduce-scatter.2.cloned.1.call-start
  7.2 1.1 copy-done
  8.3 2.2 %convolution_convert_fusion = bf16[1024,1792]{1,0:T(8,128)(2,1)S(1)} fusion(bf16[256,1024]{1,0:T(8,128)(2,1)} %param.5, bf16[256,1792]{1,0:T(8,128)(2,1)S(1)} %copy-done), kind=kOutput, calls=%fused_computation | convolution fusion | flops 941359104 | bytes 5111808 | tf_op jit(solution)/shard_map/dot_general | solution.py:35
  10.6 2.1 %copy.13 = bf16[16,2,32,1792]{3,2,1,0:T(8,128)(2,1)} copy(bf16[16,2,32,1792]{3,2,0,1:T(8,128)(2,1)S(1)} %bitcast.24) | data formatting | bytes 7340032 | tf_op jit(solution)/shard_map/transpose | solution.py:38
  12.7 0.0 reduce-scatter.2.cloned.1.call-update
  12.7 0.0 all-gather.3.cloned.1.call-start
  12.7 83.8 %reduce-scatter.2.cloned.1.call-done = bf16[2,32,1792]{2,1,0:T(8,128)(2,1)} async-done(((bf16[32,32,1792]{2,1,0:T(8,128)(2,1)}), bf16[2,32,1792]{2,1,0:T(8,128)(2,1)}) %reduce-scatter.2.cloned.1.call-update) | async-done | bytes 229392 | tf_op jit(solution)/shard_map/reduce_scatter | solution.py:39
  96.6 7.0 %all_to_all.5 = bf16[2,32,1792]{2,1,0:T(8,128)(2,1)S(1)} all-to-all(bf16[2,32,1792]{2,1,0:T(8,128)(2,1)} %reduce-scatter.2.cloned.1.call-done), channel_id=1, replica_groups=mesh['row_0'=2,'row_1'=16,'col_0'=4,'col_1'=2,'col_2'=2] {'row_0'}, dimensions={0} | all-to-all | bytes 458752 | tf_op jit(solution)/shard_map/all_to_all | solution.py:29
  103.6 0.0 copy-done.4
  103.6 0.0 copy-done.5
  103.6 0.8 multiply_reduce_fusion
  104.4 0.1 fusion.4
  104.5 5.6 %all-gather = bf16[64,1792]{1,0:T(8,128)(2,1)} all-gather(bf16[32,1792]{1,0:T(8,128)(2,1)S(1)} %fusion.4), channel_id=2, replica_groups=mesh['row_0'=2,'row_1'=16,'col_0'=4,'col_1'=2,'col_2'=2] {'row_0'}, dimensions={0}, use_global_device_ids=true | all-gather | bytes 344064 | tf_op jit(solution)/shard_map/all_gather | solution.py:49
  110.1 0.0 all-gather.3.cloned.1.call-update
  110.1 5.6 %psum.35 = f32[]{:T(128)} all-reduce(f32[]{:T(128)} %get-tuple-element.12), channel_id=1, replica_groups=mesh['row_0'=2,'row_1'=16,'col_0'=4,'col_1'=2,'col_2'=2] {'row_0'}, use_global_device_ids=true, to_apply=%region_2.0 | all-reduce | flops 1 | bytes 8 | tf_op jit(solution)/shard_map/psum | solution.py:25
  115.7 28.9 %psum.36 = f32[]{:T(128)} all-reduce(f32[]{:T(128)} %psum.35), channel_id=1, replica_groups=mesh['row_0'=2,'row_1'=16,'col_0'=4,'col_1'=2,'col_2'=2] {'row_1'}, use_global_device_ids=true, to_apply=%region_3.0 | all-reduce | flops 1 | bytes 8 | tf_op jit(solution)/shard_map/psum | solution.py:25
  144.5 0.2 copy.14
  144.8 11.0 %psum.37 = f32[]{:T(128)} all-reduce(f32[]{:T(128)} %psum.36), channel_id=1, replica_groups=mesh['row_0'=2,'row_1'=16,'col_0'=4,'col_1'=2,'col_2'=2] {'col_0'}, use_global_device_ids=true, to_apply=%region_4.0 | all-reduce | flops 1 | bytes 8 | tf_op jit(solution)/shard_map/psum | solution.py:25
  155.8 7.1 %psum.38 = f32[]{:T(128)} all-reduce(f32[]{:T(128)} %psum.37), channel_id=1, replica_groups=mesh['row_0'=2,'row_1'=16,'col_0'=4,'col_1'=2,'col_2'=2] {'col_1'}, use_global_device_ids=true, to_apply=%region_5.0 | all-reduce | flops 1 | bytes 8 | tf_op jit(solution)/shard_map/psum | solution.py:25
  162.9 3.1 %psum.39 = f32[]{:T(128)} all-reduce(f32[]{:T(128)} %psum.38), channel_id=1, replica_groups=mesh['row_0'=2,'row_1'=16,'col_0'=4,'col_1'=2,'col_2'=2] {'col_2'}, use_global_device_ids=true, to_apply=%region_6.0 | all-reduce | flops 1 | bytes 8 | tf_op jit(solution)/shard_map/psum | solution.py:25
  166.7 19.5 %all-gather.3.cloned.1.call-done = bf16[32,32,1792]{2,1,0:T(8,128)(2,1)} async-done(((bf16[2,32,1792]{2,1,0:T(8,128)(2,1)}), bf16[32,32,1792]{2,1,0:T(8,128)(2,1)}) %all-gather.3.cloned.1.call-update) | async-done | bytes 3670032 | tf_op jit(solution)/shard_map/all_gather | solution.py:49
  186.2 3.2 %fusion.1 = bf16[256,1792]{0,1:T(8,128)(2,1)S(1)} fusion(bf16[1024,1792]{1,0:T(8,128)(2,1)} %bitcast.29, bf16[256,1024]{0,1:T(8,128)(2,1)S(1)} %bitcast.28, f32[]{:T(128)S(6)} %min_shard_map.3), kind=kOutput, calls=%fused_computation.3 | convolution fusion | flops 940441600 | bytes 5111812 | tf_op jit(solution)/shard_map/dot_general | solution.py:55
  189.5 1.4 copy.16
  (10 shorter events, 0.1 us)
Async XLA Ops:
  7.2 1.2 copy-start
  7.2 89.4 %reduce-scatter.2.cloned.1.call-start = ((), (), s32[]{:S(2)}) async-start(), calls=%async_computation.2 | async-start | bytes 3899392 | tf_op jit(solution)/shard_map/reduce_scatter | solution.py:39
  12.7 90.9 %copy-start.4 = (f32[32,1792]{1,0:T(8,128)S(1)}, f32[32,1792]{1,0:T(8,128)}, u32[]{:S(2)}) copy-start(f32[32,1792]{1,0:T(8,128)} %param.6) | copy-start | bytes 688132
  12.7 91.0 %copy-start.5 = (f32[32,1792]{1,0:T(8,128)S(1)}, f32[32,1792]{1,0:T(8,128)}, u32[]{:S(2)}) copy-start(f32[32,1792]{1,0:T(8,128)} %param.7) | copy-start | bytes 688132
  12.7 131.9 %copy-start.1 = (bf16[256,1024]{1,0:T(8,128)(2,1)S(1)}, bf16[256,1024]{1,0:T(8,128)(2,1)}, u32[]{:S(2)}) copy-start(bf16[256,1024]{1,0:T(8,128)(2,1)} %param.5) | copy-start | bytes 1572868
  12.7 173.5 %all-gather.3.cloned.1.call-start = ((), (), s32[]{:S(2)}) async-start(), calls=%async_computation.3 | async-start | bytes 3899392 | tf_op jit(solution)/shard_map/all_gather | solution.py:49
  104.4 85.0 %copy-start.2 = (f32[32,1792]{1,0:T(8,128)}, f32[32,1792]{1,0:T(8,128)S(1)}, u32[]{:S(2)}) copy-start(f32[32,1792]{1,0:T(8,128)S(1)} %get-tuple-element.13) | copy-start | bytes 688132
  104.4 85.0 %copy-start.3 = (f32[32,1792]{1,0:T(8,128)}, f32[32,1792]{1,0:T(8,128)S(1)}, u32[]{:S(2)}) copy-start(f32[32,1792]{1,0:T(8,128)S(1)} %get-tuple-element.14) | copy-start | bytes 688132
Sparse Core Ops, SparseCore 0:
  12.8 83.7 reduce-scatter.1
  110.2 75.9 all-gather.2

commit v2 on v1

v2 whole, which is shorter than its diff:
```python
import jax
import jax.numpy as jnp
from jax import lax
from jax.sharding import Mesh
from jax.sharding import PartitionSpec as P

FF = 28672
R = 1024
LANES = 128
ROW = ("x_lo", "z_hi", "z_lo")
COL = ("y", "x_hi", "core")
SQUARE = ("x_lo", "z_lo")


decay_first = 0.9
decay_second = 0.999
bias_first = 1.0 - 0.9**10
bias_second = 1.0 - 0.999**10
epsilon = 1e-08
clip_limit = 0.5


def exchanged(pieces, axes):
    return lax.all_to_all(pieces, axes, split_axis=0, concat_axis=0, tiled=True)


def spread(block, axes):
    return exchanged(jnp.broadcast_to(block, (lax.axis_size(axes), *block.shape)), axes)


def column_blocks(array, parts, width):
    rows, columns = array.shape
    array = jnp.pad(array, ((0, 0), (0, parts * width - columns)))
    return array.reshape(rows, parts, width).swapaxes(0, 1)


def side_by_side(blocks, columns):
    return blocks.swapaxes(0, 1).reshape(blocks.shape[1], -1)[:, :columns]


def summed_everywhere(value):
    value = jnp.full((8, LANES), value, jnp.float32)
    for axes in (SQUARE, "z_hi", COL):
        value = jnp.sum(spread(value, axes), axis=0)
    return value[0, 0]


def local(gradient, projector, first_moment, second_moment):
    block_rows, columns = gradient.shape
    ranks = projector.shape[1]
    rows = first_moment.shape[0]
    square = lax.axis_size(SQUARE)
    z_hi, z_lo = lax.axis_size("z_hi"), lax.axis_size("z_lo")
    width = -(-columns // (square * LANES)) * LANES
    half = ranks // 2

    basis = projector.reshape(block_rows, -1, z_hi, z_lo * rows).swapaxes(1, 2)
    basis = basis.reshape(block_rows, ranks)
    own_half = lax.dynamic_slice_in_dim(basis, lax.axis_index("core") * half, half, 1)
    halves = spread(spread(own_half, SQUARE).reshape(square * block_rows, half), "core")

    block = exchanged(column_blocks(gradient, square, width), SQUARE)
    block = block.reshape(square * block_rows, width)
    partial = jnp.concatenate(
        [
            lax.dot_general(
                halves[k], block, (((0,), (0,)), ((), ())), preferred_element_type=jnp.float32
            ).astype(jnp.bfloat16)
            for k in range(2)
        ]
    )
    summed = lax.psum_scatter(
        partial.reshape(z_hi, ranks // z_hi, width), "z_hi", scatter_dimension=0, tiled=True
    )
    lowrank = exchanged(summed.reshape(square, rows, width), SQUARE)
    lowrank = side_by_side(lowrank, columns).astype(jnp.float32)

    first_new = decay_first * first_moment + (1.0 - decay_first) * lowrank
    second_new = decay_second * second_moment + (1.0 - decay_second) * lowrank * lowrank
    direction = first_new / bias_first / (jnp.sqrt(second_new / bias_second) + epsilon)

    step = exchanged(column_blocks(direction.astype(jnp.bfloat16), square, width), SQUARE)
    step = lax.all_gather(step.reshape(square * rows, width), "z_hi", axis=0, tiled=True)
    total = summed_everywhere(jnp.sum(direction * direction))
    root_mean = jnp.sqrt(total / (R * FF) + 1e-06)
    factor = jnp.minimum(1.0, clip_limit / root_mean)
    whole = lax.optimization_barrier(jnp.concatenate([halves[0], halves[1]], axis=1))
    projected = jnp.dot(whole, step, preferred_element_type=jnp.float32)
    updates = (factor * projected).astype(jnp.bfloat16)
    updates = exchanged(updates.reshape(square, block_rows, width), SQUARE)
    return (side_by_side(updates, columns), first_new, second_new)


def solution(mesh):
    torus = Mesh(mesh.devices.reshape(2, 8, 2, 4, 2, 2), (*ROW, *COL))
    in_specs = (P(ROW, COL), P(ROW, None), P(ROW, COL), P(ROW, COL))
    out_specs = (P(ROW, COL), P(ROW, COL), P(ROW, COL))
    return jax.shard_map(local, mesh=torus, in_specs=in_specs, out_specs=out_specs, check_vma=False)
```

time: 198 us -> 205 us (1.035)
  the two profiles are of different devices: /device:TPU:2 before, /device:TPU:4 now
where the time goes in v2:
time: 205 us; the launch traced here: 204 us
  waiting for transfers between devices  93.1 us (45%)
  blocking collectives  54 us (26%)
  starting transfers between devices  22.5 us (11%)
  between operations  14.9 us (7%)
  local copies, waits for them, and re-layouts  10.8 us (5%)
  matrix products  5.16 us (3%)
  other arithmetic  3.44 us (2%)
    reduce_scatter x1, waiting for transfers between devices, local(): lax.psum_scatter(partial.reshape(z_hi, ranks // z_hi, width), 'z_hi', sca...  57.3 us
    all_to_all x5, blocking collectives, exchanged(): return lax.all_to_all(pieces, axes, split_axis=0, concat_axis=0, tiled=True)  54 us
    all_to_all x4, waiting for transfers between devices, exchanged(): return lax.all_to_all(pieces, axes, split_axis=0, concat_axis=0, tiled=True)  29.8 us
    all_to_all x4, starting transfers between devices, exchanged(): return lax.all_to_all(pieces, axes, split_axis=0, concat_axis=0, tiled=True)  22.4 us
    all_gather x1, waiting for transfers between devices, local(): lax.all_gather(step.reshape(square * rows, width), 'z_hi', axis=0, tiled=...  6 us
  transfers between devices with their start and end apart: 6, of which 6 were waited for; matrix products, arithmetic and copies ran while one was open for 3% of the time, Pallas kernels for 0%

profile of v2, /device:TPU:4, one launch (start us, length us, event | category | flops | bytes accessed | tf_op | source)
XLA Modules:
  0.0 203.9 jit_solution(18431546739833409747)
XLA Ops:
  7.2 1.2 copy.37
  8.7 1.0 broadcast_in_dim.12
  9.7 3.8 %all-to-all-start = ((bf16[4,256,512]{2,1,0:T(8,128)(2,1)}), bf16[4,256,512]{2,1,0:T(8,128)(2,1)S(1)}, u32[]{:S(2)}, u32[]{:S(2)}) async-start(bf16[4,256,512]{2,1,0:T(8,128)(2,1)} %broadcast_in_dim.12), calls=%async_computation | async-start | bytes 2097152 | tf_op jit(solution)/shard_map/all_to_all | solution.py:24
  14.1 13.1 %all-to-all-done = bf16[4,256,512]{2,1,0:T(8,128)(2,1)S(1)} async-done(((bf16[4,256,512]{2,1,0:T(8,128)(2,1)}), bf16[4,256,512]{2,1,0:T(8,128)(2,1)S(1)}, u32[]{:S(2)}, u32[]{:S(2)}) %all-to-all-start) | async-done | bytes 1048608 | tf_op jit(solution)/shard_map/all_to_all | solution.py:24
  27.3 15.9 %all_to_all.45 = bf16[4,256,512]{1,2,0:T(8,128)(2,1)S(1)} all-to-all(bf16[4,256,512]{1,2,0:T(8,128)(2,1)S(1)} %bitcast.33), channel_id=1, replica_groups=mesh['x_lo'=2,'z_hi'=8,'z_lo'=2,'y'=4,'x_hi'=2,'core'=2] {'x_lo','z_lo'}, dimensions={0} | all-to-all | bytes 2097152 | tf_op jit(solution)/shard_map/all_to_all | solution.py:24
  43.2 1.5 broadcast_in_dim.13
  44.7 3.8 %all-to-all-start.1 = ((bf16[2,1024,512]{2,1,0:T(8,128)(2,1)}), bf16[2,1024,512]{2,1,0:T(8,128)(2,1)S(1)}, u32[]{:S(2)}, u32[]{:S(2)}) async-start(bf16[2,1024,512]{2,1,0:T(8,128)(2,1)} %broadcast_in_dim.13), calls=%async_computation.1 | async-start | bytes 4194304 | tf_op jit(solution)/shard_map/all_to_all | solution.py:24
  48.5 1.3 copy.41
  49.9 1.5 all-to-all-done.1
  51.3 2.0 convolution_convert_fusion.1
  54.1 1.0 pad_maximum_fusion.1
  55.2 57.3 %reduce-scatter.2.cloned.1.call-done = bf16[1,128,512]{2,1,0:T(8,128)(2,1)} async-done(((bf16[8,128,512]{2,1,0:T(8,128)(2,1)}), bf16[1,128,512]{2,1,0:T(8,128)(2,1)}) %reduce-scatter.2.cloned.1.call-update) | async-done | bytes 131088 | tf_op jit(solution)/shard_map/reduce_scatter | solution.py:72
  112.5 8.3 %all_to_all.46 = bf16[4,32,512]{2,1,0:T(8,128)(2,1)S(1)} all-to-all(bf16[4,32,512]{2,1,0:T(8,128)(2,1)} %bitcast.45), channel_id=1, replica_groups=mesh['x_lo'=2,'z_hi'=8,'z_lo'=2,'y'=4,'x_hi'=2,'core'=2] {'x_lo','z_lo'}, dimensions={0} | all-to-all | bytes 262144 | tf_op jit(solution)/shard_map/all_to_all | solution.py:24
  121.8 8.1 %all_to_all.47 = bf16[4,32,512]{2,1,0:T(8,128)(2,1)} all-to-all(bf16[4,32,512]{2,1,0:T(8,128)(2,1)S(1)} %copy.43), channel_id=1, replica_groups=mesh['x_lo'=2,'z_hi'=8,'z_lo'=2,'y'=4,'x_hi'=2,'core'=2] {'x_lo','z_lo'}, dimensions={0} | all-to-all | bytes 262144 | tf_op jit(solution)/shard_map/all_to_all | solution.py:24
  130.6 7.1 %all_to_all.48 = f32[4,8,128]{2,1,0:T(8,128)S(1)} all-to-all(f32[4,8,128]{2,1,0:T(8,128)S(1)} %broadcast_in_dim_broadcast_in_dim.3), channel_id=1, replica_groups=mesh['x_lo'=2,'z_hi'=8,'z_lo'=2,'y'=4,'x_hi'=2,'core'=2] {'x_lo','z_lo'}, dimensions={0} | all-to-all | bytes 32768 | tf_op jit(solution)/shard_map/all_to_all | solution.py:24
  138.3 7.5 %all-to-all-start.5 = ((f32[8,8,128]{2,1,0:T(8,128)}), f32[8,8,128]{2,1,0:T(8,128)S(1)}, u32[]{:S(2)}, u32[]{:S(2)}) async-start(f32[8,8,128]{2,1,0:T(8,128)} %broadcast_in_dim.14), calls=%async_computation.6 | async-start | bytes 65536 | tf_op jit(solution)/shard_map/all_to_all | solution.py:24
  145.8 1.2 slice_bitcast_fusion.1
  147.0 11.8 %all-to-all-done.5 = f32[8,8,128]{2,1,0:T(8,128)S(1)} async-done(((f32[8,8,128]{2,1,0:T(8,128)}), f32[8,8,128]{2,1,0:T(8,128)S(1)}, u32[]{:S(2)}, u32[]{:S(2)}) %all-to-all-start.5) | async-done | bytes 32800 | tf_op jit(solution)/shard_map/all_to_all | solution.py:24
  159.4 7.3 %all-to-all-start.6 = ((f32[16,8,128]{2,1,0:T(8,128)}), f32[16,8,128]{2,1,0:T(8,128)S(1)}, u32[]{:S(2)}, u32[]{:S(2)}) async-start(f32[16,8,128]{2,1,0:T(8,128)} %broadcast_in_dim.15), calls=%async_computation.7 | async-start | bytes 131072 | tf_op jit(solution)/shard_map/all_to_all | solution.py:24
  166.7 1.5 pad_maximum_fusion
  168.2 3.4 %all-to-all-done.6 = f32[16,8,128]{2,1,0:T(8,128)S(1)} async-done(((f32[16,8,128]{2,1,0:T(8,128)}), f32[16,8,128]{2,1,0:T(8,128)S(1)}, u32[]{:S(2)}, u32[]{:S(2)}) %all-to-all-start.6) | async-done | bytes 65568 | tf_op jit(solution)/shard_map/all_to_all | solution.py:24
  172.8 6.0 %all-gather.2.cloned.1.call-done = bf16[1024,512]{1,0:T(8,128)(2,1)} async-done(((bf16[128,512]{1,0:T(8,128)(2,1)}), bf16[1024,512]{1,0:T(8,128)(2,1)}) %all-gather.2.cloned.1.call-update) | async-done | bytes 1048592 | tf_op jit(solution)/shard_map/all_gather | solution.py:83
  178.8 2.5 %multiply_convert_fusion = bf16[1024,512]{1,0:T(8,128)(2,1)S(1)} fusion(bf16[1024,1024]{1,0:T(8,128)(2,1)S(1)} %pad_maximum_fusion, bf16[1024,512]{1,0:T(8,128)(2,1)} %all-gather.2.cloned.1.call-done, f32[]{:T(128)} %bitcast.12), kind=kOutput, calls=%fused_computation.1 | convolution fusion | flops 1074790400 | bytes 4194308 | tf_op jit(solution)/shard_map/dot_general | solution.py:88
  181.3 14.6 %all_to_all.49 = bf16[4,256,512]{2,1,0:T(8,128)(2,1)S(1)} all-to-all(bf16[4,256,512]{2,1,0:T(8,128)(2,1)S(1)} %bitcast.40), channel_id=1, replica_groups=mesh['x_lo'=2,'z_hi'=8,'z_lo'=2,'y'=4,'x_hi'=2,'core'=2] {'x_lo','z_lo'}, dimensions={0} | all-to-all | bytes 2097152 | tf_op jit(solution)/shard_map/all_to_all | solution.py:24
  (37 shorter events, 6.3 us)
Async XLA Ops:
  8.5 5.0 %copy-start.3 = (bf16[256,1792]{1,0:T(8,128)(2,1)S(1)}, bf16[256,1792]{1,0:T(8,128)(2,1)}, u32[]{:S(2)}) copy-start(bf16[256,1792]{1,0:T(8,128)(2,1)} %param.4) | copy-start | bytes 2752516
  9.7 17.6 %all-to-all-start = ((bf16[4,256,512]{2,1,0:T(8,128)(2,1)}), bf16[4,256,512]{2,1,0:T(8,128)(2,1)S(1)}, u32[]{:S(2)}, u32[]{:S(2)}) async-start(bf16[4,256,512]{2,1,0:T(8,128)(2,1)} %broadcast_in_dim.12), calls=%async_computation | async-start | bytes 2097152 | tf_op jit(solution)/shard_map/all_to_all | solution.py:24
  44.7 6.6 %all-to-all-start.1 = ((bf16[2,1024,512]{2,1,0:T(8,128)(2,1)}), bf16[2,1024,512]{2,1,0:T(8,128)(2,1)S(1)}, u32[]{:S(2)}, u32[]{:S(2)}) async-start(bf16[2,1024,512]{2,1,0:T(8,128)(2,1)} %broadcast_in_dim.13), calls=%async_computation.1 | async-start | bytes 4194304 | tf_op jit(solution)/shard_map/all_to_all | solution.py:24
  48.5 64.0 %reduce-scatter.2.cloned.1.call-start = ((), (), s32[]{:S(2)}) async-start(), calls=%async_computation.10 | async-start | bytes 1179648 | tf_op jit(solution)/shard_map/reduce_scatter | solution.py:72
  49.9 3.4 %copy-start = (bf16[4,256,512]{2,1,0:T(8,128)(2,1)S(1)}, bf16[4,256,512]{2,1,0:T(8,128)(2,1)}, u32[]{:S(2)}) copy-start(bf16[4,256,512]{2,1,0:T(8,128)(2,1)} %copy.41) | copy-start | bytes 3145732
  54.1 66.7 %copy-start.4 = (f32[32,1792]{1,0:T(8,128)S(1)}, f32[32,1792]{1,0:T(8,128)}, u32[]{:S(2)}) copy-start(f32[32,1792]{1,0:T(8,128)} %param.6) | copy-start | bytes 688132
  54.1 66.7 %copy-start.5 = (f32[32,1792]{1,0:T(8,128)S(1)}, f32[32,1792]{1,0:T(8,128)}, u32[]{:S(2)}) copy-start(f32[32,1792]{1,0:T(8,128)} %param.7) | copy-start | bytes 688132
  55.1 123.6 %all-gather.2.cloned.1.call-start = ((), (), s32[]{:S(2)}) async-start(), calls=%async_computation.11 | async-start | bytes 1179648 | tf_op jit(solution)/shard_map/all_gather | solution.py:83
  121.6 16.7 %copy-start.2 = (f32[32,1792]{1,0:T(8,128)}, f32[32,1792]{1,0:T(8,128)S(1)}, u32[]{:S(2)}) copy-start(f32[32,1792]{1,0:T(8,128)S(1)} %get-tuple-element.5) | copy-start | bytes 688132
  121.6 25.4 %copy-start.1 = (f32[32,1792]{1,0:T(8,128)}, f32[32,1792]{1,0:T(8,128)S(1)}, u32[]{:S(2)}) copy-start(f32[32,1792]{1,0:T(8,128)S(1)} %get-tuple-element.4) | copy-start | bytes 688132
  138.3 20.5 %all-to-all-start.5 = ((f32[8,8,128]{2,1,0:T(8,128)}), f32[8,8,128]{2,1,0:T(8,128)S(1)}, u32[]{:S(2)}, u32[]{:S(2)}) async-start(f32[8,8,128]{2,1,0:T(8,128)} %broadcast_in_dim.14), calls=%async_computation.6 | async-start | bytes 65536 | tf_op jit(solution)/shard_map/all_to_all | solution.py:24
  159.4 12.1 %all-to-all-start.6 = ((f32[16,8,128]{2,1,0:T(8,128)}), f32[16,8,128]{2,1,0:T(8,128)S(1)}, u32[]{:S(2)}, u32[]{:S(2)}) async-start(f32[16,8,128]{2,1,0:T(8,128)} %broadcast_in_dim.15), calls=%async_computation.7 | async-start | bytes 131072 | tf_op jit(solution)/shard_map/all_to_all | solution.py:24
Sparse Core Ops, SparseCore 0:
  55.3 57.1 reduce-scatter.1
  130.0 48.7 all-gather.1

commit v3 on v2

--- a/solution.py
+++ b/solution.py
@@ -38,6 +38,11 @@
     return blocks.swapaxes(0, 1).reshape(blocks.shape[1], -1)[:, :columns]
 
 
+def rank_order(basis, split, order):
+    basis = basis.reshape(-1, *split).transpose(0, *(1 + axis for axis in order))
+    return basis.reshape(basis.shape[0], -1)
+
+
 def summed_everywhere(value):
     value = jnp.full((8, LANES), value, jnp.float32)
     for axes in (SQUARE, "z_hi", COL):
@@ -50,31 +55,26 @@
     ranks = projector.shape[1]
     rows = first_moment.shape[0]
     square = lax.axis_size(SQUARE)
-    z_hi, z_lo = lax.axis_size("z_hi"), lax.axis_size("z_lo")
+    x_lo, z_hi, z_lo = (lax.axis_size(a) for a in ROW)
     width = -(-columns // (square * LANES)) * LANES
     half = ranks // 2
 
-    basis = projector.reshape(block_rows, -1, z_hi, z_lo * rows).swapaxes(1, 2)
-    basis = basis.reshape(block_rows, ranks)
+    ordered = rank_order(projector, (x_lo, z_hi, z_lo, rows), (1, 2, 0, 3))
+    partial = lax.dot_general(
+        ordered, gradient, (((0,), (0,)), ((), ())), preferred_element_type=jnp.float32
+    ).astype(jnp.bfloat16)
+    partial, projector = lax.optimization_barrier((partial, projector))
+    pieces = partial.reshape(z_hi * z_lo * x_lo, rows, columns)
+    pieces = lax.psum_scatter(pieces, ("z_hi", "z_lo"), scatter_dimension=0, tiled=True)
+
+    basis = rank_order(projector, (x_lo, z_hi, z_lo, rows), (1, 0, 2, 3))
     own_half = lax.dynamic_slice_in_dim(basis, lax.axis_index("core") * half, half, 1)
     halves = spread(spread(own_half, SQUARE).reshape(square * block_rows, half), "core")
+    whole = jnp.concatenate([halves[0], halves[1]], axis=1)
+    pieces, whole = lax.optimization_barrier((pieces, whole))
 
-    block = exchanged(column_blocks(gradient, square, width), SQUARE)
-    block = block.reshape(square * block_rows, width)
-    partial = jnp.concatenate(
-        [
-            lax.dot_general(
-                halves[k], block, (((0,), (0,)), ((), ())), preferred_element_type=jnp.float32
-            ).astype(jnp.bfloat16)
-            for k in range(2)
-        ]
-    )
-    summed = lax.psum_scatter(
-        partial.reshape(z_hi, ranks // z_hi, width), "z_hi", scatter_dimension=0, tiled=True
-    )
-    lowrank = exchanged(summed.reshape(square, rows, width), SQUARE)
-    lowrank = side_by_side(lowrank, columns).astype(jnp.float32)
-
+    pair = exchanged(pieces, "x_lo").astype(jnp.float32)
+    lowrank = pair[0] + pair[1]
     first_new = decay_first * first_moment + (1.0 - decay_first) * lowrank
     second_new = decay_second * second_moment + (1.0 - decay_second) * lowrank * lowrank
     direction = first_new / bias_first / (jnp.sqrt(second_new / bias_second) + epsilon)
@@ -84,7 +84,6 @@
     total = summed_everywhere(jnp.sum(direction * direction))
     root_mean = jnp.sqrt(total / (R * FF) + 1e-06)
     factor = jnp.minimum(1.0, clip_limit / root_mean)
-    whole = lax.optimization_barrier(jnp.concatenate([halves[0], halves[1]], axis=1))
     projected = jnp.dot(whole, step, preferred_element_type=jnp.float32)
     updates = (factor * projected).astype(jnp.bfloat16)
     updates = exchanged(updates.reshape(square, block_rows, width), SQUARE)

time: 205 us -> 193 us (0.941)
  the two profiles are of different devices: /device:TPU:4 before, /device:TPU:16 now
where the time goes in v3:
time: 193 us
  blocking collectives  95.9 us (50%)
  waiting for transfers between devices  65.4 us (34%)
  between operations  14.9 us (8%)
  local copies, waits for them, and re-layouts  8.62 us (4%)
  matrix products  5.39 us (3%)
  other arithmetic  2.33 us (1%)
    all_to_all x8, blocking collectives, exchanged(): return lax.all_to_all(pieces, axes, split_axis=0, concat_axis=0, tiled=True)  95.9 us
    reduce_scatter x1, waiting for transfers between devices, local(): lax.psum_scatter(pieces, ('z_hi', 'z_lo'), scatter_dimension=0, tiled=True)  58.3 us
    all_gather x1, waiting for transfers between devices, local(): lax.all_gather(step.reshape(square * rows, width), 'z_hi', axis=0, tiled=...  7.01 us
  transfers between devices with their start and end apart: 2, of which 2 were waited for; matrix products, arithmetic and copies ran while one was open for 1% of the time, Pallas kernels for 0%

profile of v3, /device:TPU:16, one launch (start us, length us, event | category | flops | bytes accessed | tf_op | source)
XLA Modules:
  0.0 192.6 jit_solution(4110589949087193565)
XLA Ops:
  7.2 1.3 copy.28
  8.6 2.9 %convolution_convert_fusion = bf16[1024,1792]{1,0:T(8,128)(2,1)} fusion(bf16[256,1024]{0,1:T(8,128)(2,1)S(1)} %bitcast.36, bf16[256,1792]{1,0:T(8,128)(2,1)S(1)} %copy-done), kind=kOutput, calls=%fused_computation | convolution fusion | flops 941359104 | bytes 5111808 | tf_op jit(solution)/shard_map/dot_general | solution.py:63
  11.6 1.0 copy-done.1
  12.6 0.2 copy.30
  12.9 0.1 copy.32
  13.1 18.1 %all_to_all.40 = bf16[4,256,512]{2,1,0:T(8,128)(2,1)S(1)} all-to-all(bf16[4,256,512]{2,1,0:T(8,128)(2,1)S(1)} %broadcast_in_dim.12), channel_id=1, replica_groups=mesh['x_lo'=2,'z_hi'=8,'z_lo'=2,'y'=4,'x_hi'=2,'core'=2] {'x_lo','z_lo'}, dimensions={0} | all-to-all | bytes 2097152 | tf_op jit(solution)/shard_map/all_to_all | solution.py:24
  31.3 5.4 %all_to_all.41 = bf16[2,1024,512]{2,1,0:T(8,128)(2,1)S(1)} all-to-all(bf16[2,1024,512]{2,1,0:T(8,128)(2,1)S(1)} %broadcast_in_dim.13), channel_id=1, replica_groups=mesh['x_lo'=2,'z_hi'=8,'z_lo'=2,'y'=4,'x_hi'=2,'core'=2] {'core'}, dimensions={0} | all-to-all | bytes 4194304 | tf_op jit(solution)/shard_map/all_to_all | solution.py:24
  36.8 0.3 pad_maximum_fusion
  37.1 58.3 %reduce-scatter.2.cloned.1.call-done = bf16[2,32,1792]{2,1,0:T(8,128)(2,1)} async-done(((bf16[32,32,1792]{2,1,0:T(8,128)(2,1)}), bf16[2,32,1792]{2,1,0:T(8,128)(2,1)}) %reduce-scatter.2.cloned.1.call-update) | async-done | bytes 229392 | tf_op jit(solution)/shard_map/reduce_scatter | solution.py:68
  95.4 8.6 %all_to_all.42 = bf16[2,32,1792]{2,1,0:T(8,128)(2,1)S(1)} all-to-all(bf16[2,32,1792]{2,1,0:T(8,128)(2,1)} %reduce-scatter.2.cloned.1.call-done), channel_id=1, replica_groups=mesh['x_lo'=2,'z_hi'=8,'z_lo'=2,'y'=4,'x_hi'=2,'core'=2] {'x_lo'}, dimensions={0} | all-to-all | bytes 458752 | tf_op jit(solution)/shard_map/all_to_all | solution.py:24
  104.1 1.9 multiply_reduce_fusion
  106.1 0.7 pad.4
  106.8 1.6 reshape.50
  108.4 0.9 copy.33
  109.3 8.1 %all_to_all.43 = bf16[4,32,512]{2,1,0:T(8,128)(2,1)} all-to-all(bf16[4,32,512]{2,1,0:T(8,128)(2,1)S(1)} %copy.33), channel_id=1, replica_groups=mesh['x_lo'=2,'z_hi'=8,'z_lo'=2,'y'=4,'x_hi'=2,'core'=2] {'x_lo','z_lo'}, dimensions={0} | all-to-all | bytes 262144 | tf_op jit(solution)/shard_map/all_to_all | solution.py:24
  117.4 0.6 broadcast_in_dim_broadcast_in_dim.3
  118.1 7.1 %all_to_all.44 = f32[4,8,128]{2,1,0:T(8,128)S(1)} all-to-all(f32[4,8,128]{2,1,0:T(8,128)S(1)} %broadcast_in_dim_broadcast_in_dim.3), channel_id=1, replica_groups=mesh['x_lo'=2,'z_hi'=8,'z_lo'=2,'y'=4,'x_hi'=2,'core'=2] {'x_lo','z_lo'}, dimensions={0} | all-to-all | bytes 32768 | tf_op jit(solution)/shard_map/all_to_all | solution.py:24
  125.1 21.5 %all_to_all.45 = f32[8,8,128]{2,1,0:T(8,128)S(1)} all-to-all(f32[8,8,128]{2,1,0:T(8,128)S(1)} %broadcast_in_dim.14), channel_id=1, replica_groups=mesh['x_lo'=2,'z_hi'=8,'z_lo'=2,'y'=4,'x_hi'=2,'core'=2] {'z_hi'}, dimensions={0} | all-to-all | bytes 65536 | tf_op jit(solution)/shard_map/all_to_all | solution.py:24
  146.7 12.6 %all_to_all.46 = f32[16,8,128]{2,1,0:T(8,128)S(1)} all-to-all(f32[16,8,128]{2,1,0:T(8,128)S(1)} %broadcast_in_dim.15), channel_id=1, replica_groups=mesh['x_lo'=2,'z_hi'=8,'z_lo'=2,'y'=4,'x_hi'=2,'core'=2] {'y','x_hi','co..., dimensions={0} | all-to-all | bytes 131072 | tf_op jit(solution)/shard_map/all_to_all | solution.py:24
  159.3 0.5 slice.22
  160.5 7.0 %all-gather.2.cloned.1.call-done = bf16[1024,512]{1,0:T(8,128)(2,1)} async-done(((bf16[128,512]{1,0:T(8,128)(2,1)}), bf16[1024,512]{1,0:T(8,128)(2,1)}) %all-gather.2.cloned.1.call-update) | async-done | bytes 1048592 | tf_op jit(solution)/shard_map/all_gather | solution.py:83
  167.5 2.5 %multiply_convert_fusion = bf16[1024,512]{1,0:T(8,128)(2,1)S(1)} fusion(bf16[1024,1024]{1,0:T(8,128)(2,1)S(1)} %pad_maximum_fusion, bf16[1024,512]{1,0:T(8,128)(2,1)} %all-gather.2.cloned.1.call-done, f32[]{:T(128)} %bitcast.11), kind=kOutput, calls=%fused_computation.2 | convolution fusion | flops 1074790400 | bytes 4194308 | tf_op jit(solution)/shard_map/dot_general | solution.py:87
  170.0 14.7 %all_to_all.47 = bf16[4,256,512]{2,1,0:T(8,128)(2,1)S(1)} all-to-all(bf16[4,256,512]{2,1,0:T(8,128)(2,1)S(1)} %bitcast.41), channel_id=1, replica_groups=mesh['x_lo'=2,'z_hi'=8,'z_lo'=2,'y'=4,'x_hi'=2,'core'=2] {'x_lo','z_lo'}, dimensions={0} | all-to-all | bytes 2097152 | tf_op jit(solution)/shard_map/all_to_all | solution.py:24
  184.8 1.0 slice.28
  (25 shorter events, 0.9 us)
Async XLA Ops:
  7.2 1.4 copy-start
  7.2 88.3 %reduce-scatter.2.cloned.1.call-start = ((), (), s32[]{:S(2)}) async-start(), calls=%async_computation.9 | async-start | bytes 3899392 | tf_op jit(solution)/shard_map/reduce_scatter | solution.py:68
  11.5 1.0 copy-start.1
  11.5 155.9 %all-gather.2.cloned.1.call-start = ((), (), s32[]{:S(2)}) async-start(), calls=%async_computation.10 | async-start | bytes 1179648 | tf_op jit(solution)/shard_map/all_gather | solution.py:83
  106.0 64.0 %copy-start.2 = (f32[32,1792]{1,0:T(8,128)}, f32[32,1792]{1,0:T(8,128)S(1)}, u32[]{:S(2)}) copy-start(f32[32,1792]{1,0:T(8,128)S(1)} %get-tuple-element.12) | copy-start | bytes 688132
  106.0 64.0 %copy-start.3 = (f32[32,1792]{1,0:T(8,128)}, f32[32,1792]{1,0:T(8,128)S(1)}, u32[]{:S(2)}) copy-start(f32[32,1792]{1,0:T(8,128)S(1)} %get-tuple-element.13) | copy-start | bytes 688132
Sparse Core Ops, SparseCore 0:
  11.7 83.7 reduce-scatter.1
  117.5 49.8 all-gather.1

commit v4 on v3

--- a/solution.py
+++ b/solution.py
@@ -1,3 +1,5 @@
+import functools
+
 import jax
 import jax.numpy as jnp
 from jax import lax
@@ -38,9 +40,11 @@
     return blocks.swapaxes(0, 1).reshape(blocks.shape[1], -1)[:, :columns]
 
 
-def rank_order(basis, split, order):
-    basis = basis.reshape(-1, *split).transpose(0, *(1 + axis for axis in order))
-    return basis.reshape(basis.shape[0], -1)
+def adam(lowrank, first_moment, second_moment):
+    first_new = decay_first * first_moment + (1.0 - decay_first) * lowrank
+    second_new = decay_second * second_moment + (1.0 - decay_second) * lowrank * lowrank
+    direction = first_new / bias_first / (jnp.sqrt(second_new / bias_second) + epsilon)
+    return first_new, second_new, direction
 
 
 def summed_everywhere(value):
@@ -59,29 +63,39 @@
     width = -(-columns // (square * LANES)) * LANES
     half = ranks // 2
 
-    ordered = rank_order(projector, (x_lo, z_hi, z_lo, rows), (1, 2, 0, 3))
+    split = (ranks // (z_hi * z_lo * rows), z_hi * z_lo, rows)
+    ordered = projector.reshape(block_rows, *split).swapaxes(1, 2).reshape(block_rows, ranks)
     partial = lax.dot_general(
         ordered, gradient, (((0,), (0,)), ((), ())), preferred_element_type=jnp.float32
     ).astype(jnp.bfloat16)
-    partial, projector = lax.optimization_barrier((partial, projector))
+    partial, ordered, first_moment, second_moment = lax.optimization_barrier(
+        (partial, ordered, first_moment, second_moment)
+    )
     pieces = partial.reshape(z_hi * z_lo * x_lo, rows, columns)
     pieces = lax.psum_scatter(pieces, ("z_hi", "z_lo"), scatter_dimension=0, tiled=True)
 
-    basis = rank_order(projector, (x_lo, z_hi, z_lo, rows), (1, 0, 2, 3))
-    own_half = lax.dynamic_slice_in_dim(basis, lax.axis_index("core") * half, half, 1)
+    own_half = lax.dynamic_slice_in_dim(ordered, lax.axis_index("core") * half, half, 1)
     halves = spread(spread(own_half, SQUARE).reshape(square * block_rows, half), "core")
     whole = jnp.concatenate([halves[0], halves[1]], axis=1)
-    pieces, whole = lax.optimization_barrier((pieces, whole))
+    moments = jnp.concatenate([first_moment, second_moment])
+    moments = exchanged(column_blocks(moments, square, width), SQUARE)
+    moments = moments.reshape(x_lo, z_lo, 2, rows, width).transpose(2, 1, 0, 3, 4)
+    pieces, whole, moments = lax.optimization_barrier((pieces, whole, moments))
+
+    quarter = exchanged(column_blocks(pieces.reshape(x_lo * rows, columns), square, width), SQUARE)
+    quarter = quarter.reshape(x_lo, z_lo, x_lo, rows, width).astype(jnp.float32)
+    quarter = functools.reduce(jnp.add, [quarter[k] for k in range(x_lo)])
+    direction = adam(quarter, moments[0], moments[1])[2]
+    step = direction.astype(jnp.bfloat16).reshape(square * rows, width)
+    step, pieces = lax.optimization_barrier((step, pieces))
+    step = lax.all_gather(step, "z_hi", axis=0, tiled=True)
+    total = summed_everywhere(jnp.sum(direction * direction))
 
     pair = exchanged(pieces, "x_lo").astype(jnp.float32)
-    lowrank = pair[0] + pair[1]
-    first_new = decay_first * first_moment + (1.0 - decay_first) * lowrank
-    second_new = decay_second * second_moment + (1.0 - decay_second) * lowrank * lowrank
-    direction = first_new / bias_first / (jnp.sqrt(second_new / bias_second) + epsilon)
+    first_new, second_new, _ = adam(
+        functools.reduce(jnp.add, [pair[k] for k in range(x_lo)]), first_moment, second_moment
+    )
 
-    step = exchanged(column_blocks(direction.astype(jnp.bfloat16), square, width), SQUARE)
-    step = lax.all_gather(step.reshape(square * rows, width), "z_hi", axis=0, tiled=True)
-    total = summed_everywhere(jnp.sum(direction * direction))
     root_mean = jnp.sqrt(total / (R * FF) + 1e-06)
     factor = jnp.minimum(1.0, clip_limit / root_mean)
     projected = jnp.dot(whole, step, preferred_element_type=jnp.float32)

time: 193 us -> 189 us (0.979)
  the two profiles are of different devices: /device:TPU:16 before, /device:TPU:1 now
where the time goes in v4:
time: 189 us; the launch traced here: 188 us
  waiting for transfers between devices  69.8 us (37%)
  blocking collectives  64.9 us (34%)
  starting transfers between devices  18.7 us (10%)
  between operations  15 us (8%)
  local copies, waits for them, and re-layouts  8.45 us (4%)
  matrix products  6.99 us (4%)
  other arithmetic  4.28 us (2%)
    all_to_all x4, blocking collectives, exchanged(): return lax.all_to_all(pieces, axes, split_axis=0, concat_axis=0, tiled=True)  64.9 us
    reduce_scatter x1, waiting for transfers between devices, local(): lax.psum_scatter(pieces, ('z_hi', 'z_lo'), scatter_dimension=0, tiled=True)  35.7 us
    all_to_all x5, waiting for transfers between devices, exchanged(): return lax.all_to_all(pieces, axes, split_axis=0, concat_axis=0, tiled=True)  34.1 us
    all_to_all x5, starting transfers between devices, exchanged(): return lax.all_to_all(pieces, axes, split_axis=0, concat_axis=0, tiled=True)  18.6 us
    dot_general x1, matrix products, local(): projected = jnp.dot(whole, step, preferred_element_type=jnp.float32)  4.09 us
  transfers between devices with their start and end apart: 7, of which 5 were waited for; matrix products, arithmetic and copies ran while one was open for 6% of the time, Pallas kernels for 0%

profile of v4, /device:TPU:1, one launch (start us, length us, event | category | flops | bytes accessed | tf_op | source)
XLA Modules:
  0.0 188.1 jit_solution(1043714054918294577)
XLA Ops:
  7.2 1.3 copy.48
  8.6 2.9 %convolution_convert_fusion = bf16[1024,1792]{1,0:T(8,128)(2,1)} fusion(bf16[256,1024]{0,1:T(8,128)(2,1)S(1)} %bitcast.64, bf16[256,1792]{1,0:T(8,128)(2,1)S(1)} %copy-done), kind=kOutput, calls=%fused_computation | convolution fusion | flops 941359104 | bytes 5111808 | tf_op jit(solution)/shard_map/dot_general | solution.py:68
  11.7 1.1 broadcast_in_dim.12
  12.8 4.7 %all-to-all-start = ((bf16[4,256,512]{2,1,0:T(8,128)(2,1)}), bf16[4,256,512]{2,1,0:T(8,128)(2,1)S(1)}, u32[]{:S(2)}, u32[]{:S(2)}) async-start(bf16[4,256,512]{2,1,0:T(8,128)(2,1)} %broadcast_in_dim.12), calls=%async_computation.1 | async-start | bytes 2097152 | tf_op jit(solution)/shard_map/all_to_all | solution.py:26
  17.9 1.0 copy.51
  18.8 6.9 %all-to-all-done = bf16[4,256,512]{2,1,0:T(8,128)(2,1)S(1)} async-done(((bf16[4,256,512]{2,1,0:T(8,128)(2,1)}), bf16[4,256,512]{2,1,0:T(8,128)(2,1)S(1)}, u32[]{:S(2)}, u32[]{:S(2)}) %all-to-all-start) | async-done | bytes 1048608 | tf_op jit(solution)/shard_map/all_to_all | solution.py:26
  25.9 11.9 %all_to_all.45 = bf16[2,1024,512]{2,1,0:T(8,128)(2,1)S(1)} all-to-all(bf16[2,1024,512]{2,1,0:T(8,128)(2,1)S(1)} %broadcast_in_dim.13), channel_id=1, replica_groups=mesh['x_lo'=2,'z_hi'=8,'z_lo'=2,'y'=4,'x_hi'=2,'core'=2] {'core'}, dimensions={0} | all-to-all | bytes 4194304 | tf_op jit(solution)/shard_map/all_to_all | solution.py:26
  37.8 3.5 %all-to-all-start.2 = ((f32[4,64,512]{2,1,0:T(8,128)}), f32[4,64,512]{2,1,0:T(8,128)S(1)}, u32[]{:S(2)}, u32[]{:S(2)}) async-start(f32[4,64,512]{2,1,0:T(8,128)} %copy.51), calls=%async_computation.3 | async-start | bytes 1048576 | tf_op jit(solution)/shard_map/all_to_all | solution.py:26
  41.4 1.6 pad_maximum_fusion
  43.0 11.0 %all-to-all-done.2 = f32[4,64,512]{2,1,0:T(8,128)S(1)} async-done(((f32[4,64,512]{2,1,0:T(8,128)}), f32[4,64,512]{2,1,0:T(8,128)S(1)}, u32[]{:S(2)}, u32[]{:S(2)}) %all-to-all-start.2) | async-done | bytes 524320 | tf_op jit(solution)/shard_map/all_to_all | solution.py:26
  54.0 35.7 %reduce-scatter.2.cloned.1.call-done = bf16[2,32,1792]{2,1,0:T(8,128)(2,1)} async-done(((bf16[32,32,1792]{2,1,0:T(8,128)(2,1)}), bf16[2,32,1792]{2,1,0:T(8,128)(2,1)}) %reduce-scatter.2.cloned.1.call-update) | async-done | bytes 229392 | tf_op jit(solution)/shard_map/reduce_scatter | solution.py:75
  89.6 1.0 pad.9
  91.5 3.4 %all-to-all-start.3 = ((bf16[4,64,512]{2,1,0:T(8,128)(2,1)}), bf16[4,64,512]{2,1,0:T(8,128)(2,1)S(1)}, u32[]{:S(2)}, u32[]{:S(2)}) async-start(bf16[4,64,512]{2,1,0:T(8,128)(2,1)} %copy.53), calls=%async_computation.4 | async-start | bytes 524288 | tf_op jit(solution)/shard_map/all_to_all | solution.py:26
  95.1 4.0 %all-to-all-done.3 = bf16[4,64,512]{2,1,0:T(8,128)(2,1)S(1)} async-done(((bf16[4,64,512]{2,1,0:T(8,128)(2,1)}), bf16[4,64,512]{2,1,0:T(8,128)(2,1)S(1)}, u32[]{:S(2)}, u32[]{:S(2)}) %all-to-all-start.3) | async-done | bytes 262176 | tf_op jit(solution)/shard_map/all_to_all | solution.py:26
  99.2 0.8 fusion.14
  101.5 5.9 %all_to_all.46 = f32[4,8,128]{2,1,0:T(8,128)S(1)} all-to-all(f32[4,8,128]{2,1,0:T(8,128)S(1)} %broadcast_in_dim_broadcast_in_dim.3), channel_id=1, replica_groups=mesh['x_lo'=2,'z_hi'=8,'z_lo'=2,'y'=4,'x_hi'=2,'core'=2] {'x_lo','z_lo'}, dimensions={0} | all-to-all | bytes 32768 | tf_op jit(solution)/shard_map/all_to_all | solution.py:26
  107.4 19.3 %all_to_all.47 = f32[8,8,128]{2,1,0:T(8,128)S(1)} all-to-all(f32[8,8,128]{2,1,0:T(8,128)S(1)} %broadcast_in_dim.14), channel_id=1, replica_groups=mesh['x_lo'=2,'z_hi'=8,'z_lo'=2,'y'=4,'x_hi'=2,'core'=2] {'z_hi'}, dimensions={0} | all-to-all | bytes 65536 | tf_op jit(solution)/shard_map/all_to_all | solution.py:26
  126.8 27.7 %all_to_all.48 = f32[16,8,128]{2,1,0:T(8,128)S(1)} all-to-all(f32[16,8,128]{2,1,0:T(8,128)S(1)} %broadcast_in_dim.15), channel_id=1, replica_groups=mesh['x_lo'=2,'z_hi'=8,'z_lo'=2,'y'=4,'x_hi'=2,'core'=2] {'y','x_hi','co..., dimensions={0} | all-to-all | bytes 131072 | tf_op jit(solution)/shard_map/all_to_all | solution.py:26
  154.5 3.4 %all-to-all-start.8 = ((bf16[2,32,1792]{2,1,0:T(8,128)(2,1)}), bf16[2,32,1792]{2,1,0:T(8,128)(2,1)S(1)}, u32[]{:S(2)}, u32[]{:S(2)}) async-start(bf16[2,32,1792]{2,1,0:T(8,128)(2,1)} %reduce-scatter.2.cloned.1.call-done), calls=%async_computation.9 | async-start | bytes 458752 | tf_op jit(solution)/shard_map/all_to_all | solution.py:26
  159.2 4.1 %multiply_convert_fusion = bf16[1024,512]{1,0:T(8,128)(2,1)} fusion(bf16[1024,1024]{1,0:T(8,128)(2,1)} %pad_maximum_fusion, bf16[1024,512]{1,0:T(8,128)(2,1)} %all-gather.2.cloned.1.call-done, f32[]{:T(128)} %bitcast.15), kind=kOutput, calls=%fused_computation.2 | convolution fusion | flops 1074790400 | bytes 4194308 | tf_op jit(solution)/shard_map/dot_general | solution.py:101
  163.3 3.7 %all-to-all-start.7 = ((bf16[4,256,512]{2,1,0:T(8,128)(2,1)}), bf16[4,256,512]{2,1,0:T(8,128)(2,1)S(1)}, u32[]{:S(2)}, u32[]{:S(2)}) async-start(bf16[4,256,512]{2,1,0:T(8,128)(2,1)} %bitcast.19), calls=%async_computation.8 | async-start | bytes 2097152 | tf_op jit(solution)/shard_map/all_to_all | solution.py:26
  167.1 0.8 fusion.16
  167.9 12.2 %all-to-all-done.7 = bf16[4,256,512]{2,1,0:T(8,128)(2,1)S(1)} async-done(((bf16[4,256,512]{2,1,0:T(8,128)(2,1)}), bf16[4,256,512]{2,1,0:T(8,128)(2,1)S(1)}, u32[]{:S(2)}, u32[]{:S(2)}) %all-to-all-start.7) | async-done | bytes 1048608 | tf_op jit(solution)/shard_map/all_to_all | solution.py:26
  180.2 1.0 slice.47
  (41 shorter events, 4.3 us)
Async XLA Ops:
  7.2 1.4 copy-start
  7.2 82.4 %reduce-scatter.2.cloned.1.call-start = ((), (), s32[]{:S(2)}) async-start(), calls=%async_computation.10 | async-start | bytes 3899392 | tf_op jit(solution)/shard_map/reduce_scatter | solution.py:75
  11.6 5.9 %copy-start.1 = (f32[32,1792]{1,0:T(8,128)S(1)}, f32[32,1792]{1,0:T(8,128)}, u32[]{:S(2)}) copy-start(f32[32,1792]{1,0:T(8,128)} %param.7) | copy-start | bytes 688132
  11.6 5.9 %copy-start.3 = (f32[32,1792]{1,0:T(8,128)S(1)}, f32[32,1792]{1,0:T(8,128)}, u32[]{:S(2)}) copy-start(f32[32,1792]{1,0:T(8,128)} %param.6) | copy-start | bytes 688132
  12.8 12.9 %all-to-all-start = ((bf16[4,256,512]{2,1,0:T(8,128)(2,1)}), bf16[4,256,512]{2,1,0:T(8,128)(2,1)S(1)}, u32[]{:S(2)}, u32[]{:S(2)}) async-start(bf16[4,256,512]{2,1,0:T(8,128)(2,1)} %broadcast_in_dim.12), calls=%async_computation.1 | async-start | bytes 2097152 | tf_op jit(solution)/shard_map/all_to_all | solution.py:26
  37.8 16.2 %all-to-all-start.2 = ((f32[4,64,512]{2,1,0:T(8,128)}), f32[4,64,512]{2,1,0:T(8,128)S(1)}, u32[]{:S(2)}, u32[]{:S(2)}) async-start(f32[4,64,512]{2,1,0:T(8,128)} %copy.51), calls=%async_computation.3 | async-start | bytes 1048576 | tf_op jit(solution)/shard_map/all_to_all | solution.py:26
  91.5 7.6 %all-to-all-start.3 = ((bf16[4,64,512]{2,1,0:T(8,128)(2,1)}), bf16[4,64,512]{2,1,0:T(8,128)(2,1)S(1)}, u32[]{:S(2)}, u32[]{:S(2)}) async-start(bf16[4,64,512]{2,1,0:T(8,128)(2,1)} %copy.53), calls=%async_computation.4 | async-start | bytes 524288 | tf_op jit(solution)/shard_map/all_to_all | solution.py:26
  94.9 64.3 %all-gather.2.cloned.1.call-start = ((), (), s32[]{:S(2)}) async-start(), calls=%async_computation.11 | async-start | bytes 1179648 | tf_op jit(solution)/shard_map/all_gather | solution.py:91
  154.5 8.8 %all-to-all-start.8 = ((bf16[2,32,1792]{2,1,0:T(8,128)(2,1)}), bf16[2,32,1792]{2,1,0:T(8,128)(2,1)S(1)}, u32[]{:S(2)}, u32[]{:S(2)}) async-start(bf16[2,32,1792]{2,1,0:T(8,128)(2,1)} %reduce-scatter.2.cloned.1.call-done), calls=%async_computation.9 | async-start | bytes 458752 | tf_op jit(solution)/shard_map/all_to_all | solution.py:26
  163.3 3.7 %copy-start.2 = (f32[32,1792]{1,0:T(8,128)S(1)}, f32[32,1792]{1,0:T(8,128)}, u32[]{:S(2)}) copy-start(f32[32,1792]{1,0:T(8,128)} %param.7) | copy-start | bytes 688132
  163.3 3.7 %copy-start.4 = (f32[32,1792]{1,0:T(8,128)S(1)}, f32[32,1792]{1,0:T(8,128)}, u32[]{:S(2)}) copy-start(f32[32,1792]{1,0:T(8,128)} %param.6) | copy-start | bytes 688132
  163.3 16.8 %all-to-all-start.7 = ((bf16[4,256,512]{2,1,0:T(8,128)(2,1)}), bf16[4,256,512]{2,1,0:T(8,128)(2,1)S(1)}, u32[]{:S(2)}, u32[]{:S(2)}) async-start(bf16[4,256,512]{2,1,0:T(8,128)(2,1)} %bitcast.19), calls=%async_computation.8 | async-start | bytes 2097152 | tf_op jit(solution)/shard_map/all_to_all | solution.py:26
Sparse Core Ops, SparseCore 0:
  11.6 77.9 reduce-scatter.1
  100.2 56.2 all-gather.1

commit v5 on v4

--- a/solution.py
+++ b/solution.py
@@ -1,5 +1,3 @@
-import functools
-
 import jax
 import jax.numpy as jnp
 from jax import lax
@@ -62,39 +60,51 @@
     x_lo, z_hi, z_lo = (lax.axis_size(a) for a in ROW)
     width = -(-columns // (square * LANES)) * LANES
     half = ranks // 2
+    core = lax.axis_index("core")
 
-    split = (ranks // (z_hi * z_lo * rows), z_hi * z_lo, rows)
-    ordered = projector.reshape(block_rows, *split).swapaxes(1, 2).reshape(block_rows, ranks)
-    partial = lax.dot_general(
-        ordered, gradient, (((0,), (0,)), ((), ())), preferred_element_type=jnp.float32
-    ).astype(jnp.bfloat16)
-    partial, ordered, first_moment, second_moment = lax.optimization_barrier(
-        (partial, ordered, first_moment, second_moment)
+    def own_first(array, axis):
+        return jnp.where(core == 0, array, jnp.flip(array, axis))
+
+    ordered = projector.reshape(block_rows, x_lo, z_hi, z_lo, rows).transpose(0, 3, 2, 1, 4)
+    own_half = lax.dynamic_slice_in_dim(ordered.reshape(block_rows, ranks), core * half, half, 1)
+    own_half = spread(own_half, SQUARE).reshape(square * block_rows, half)
+    blocks = column_blocks(gradient, square, width)
+    own_half, blocks = lax.optimization_barrier((own_half, blocks))
+    other_half = lax.ppermute(own_half, "core", [(0, 1), (1, 0)])
+    block = exchanged(blocks, SQUARE).reshape(square * block_rows, width)
+    partial = [
+        lax.dot_general(
+            basis, block, (((0,), (0,)), ((), ())), preferred_element_type=jnp.float32
+        ).astype(jnp.bfloat16)
+        for basis in (own_half, other_half)
+    ]
+    partial = jnp.stack([p.reshape(z_hi, half // z_hi, width) for p in partial], axis=1)
+    partial = partial.reshape(z_hi, ranks // z_hi, width)
+    partial, own_half, other_half, first_moment, second_moment = lax.optimization_barrier(
+        (partial, own_half, other_half, first_moment, second_moment)
     )
-    pieces = partial.reshape(z_hi * z_lo * x_lo, rows, columns)
-    pieces = lax.psum_scatter(pieces, ("z_hi", "z_lo"), scatter_dimension=0, tiled=True)
+    summed = lax.psum_scatter(partial, "z_hi", scatter_dimension=0, tiled=True)
 
-    own_half = lax.dynamic_slice_in_dim(ordered, lax.axis_index("core") * half, half, 1)
-    halves = spread(spread(own_half, SQUARE).reshape(square * block_rows, half), "core")
-    whole = jnp.concatenate([halves[0], halves[1]], axis=1)
+    whole = jnp.stack(
+        [basis.reshape(-1, z_hi, half // z_hi) for basis in (own_half, other_half)], axis=2
+    ).reshape(square * block_rows, ranks)
     moments = jnp.concatenate([first_moment, second_moment])
     moments = exchanged(column_blocks(moments, square, width), SQUARE)
     moments = moments.reshape(x_lo, z_lo, 2, rows, width).transpose(2, 1, 0, 3, 4)
-    pieces, whole, moments = lax.optimization_barrier((pieces, whole, moments))
+    moments = own_first(moments, 1).reshape(2, square * rows, width)
+    summed, whole, moments = lax.optimization_barrier((summed, whole, moments))
 
-    quarter = exchanged(column_blocks(pieces.reshape(x_lo * rows, columns), square, width), SQUARE)
-    quarter = quarter.reshape(x_lo, z_lo, x_lo, rows, width).astype(jnp.float32)
-    quarter = functools.reduce(jnp.add, [quarter[k] for k in range(x_lo)])
-    direction = adam(quarter, moments[0], moments[1])[2]
-    step = direction.astype(jnp.bfloat16).reshape(square * rows, width)
-    step, pieces = lax.optimization_barrier((step, pieces))
+    summed = summed.reshape(square * rows, width)
+    direction = adam(summed.astype(jnp.float32), moments[0], moments[1])[2]
+    step = direction.astype(jnp.bfloat16)
+    step, summed = lax.optimization_barrier((step, summed))
     step = lax.all_gather(step, "z_hi", axis=0, tiled=True)
     total = summed_everywhere(jnp.sum(direction * direction))
 
-    pair = exchanged(pieces, "x_lo").astype(jnp.float32)
-    first_new, second_new, _ = adam(
-        functools.reduce(jnp.add, [pair[k] for k in range(x_lo)]), first_moment, second_moment
-    )
+    lowrank = own_first(summed.reshape(z_lo, x_lo, rows, width), 0).swapaxes(0, 1)
+    lowrank = exchanged(lowrank.reshape(square, rows, width), SQUARE)
+    lowrank = side_by_side(lowrank, columns).astype(jnp.float32)
+    first_new, second_new, _ = adam(lowrank, first_moment, second_moment)
 
     root_mean = jnp.sqrt(total / (R * FF) + 1e-06)
     factor = jnp.minimum(1.0, clip_limit / root_mean)

time: 189 us -> 187 us (0.989)
  blocking collectives: 64.9 us -> 24.6 us
  starting transfers between devices: 18.7 us -> 42 us
  waiting for transfers between devices: 69.8 us -> 81.3 us
  other arithmetic: 4.28 us -> 6.84 us
    all_to_all x4 -> x2, blocking collectives: 64.9 us -> 24.6 us  [exchanged(): return lax.all_to_all(pieces, axes, split_axis=0, concat_axis=0, tiled=True)]
    reduce_scatter x1, waiting for transfers between devices: 35.7 us -> 51.6 us  [local(): summed = lax.psum_scatter(partial, 'z_hi', scatter_dimension=0, tiled=True)]
    all_to_all x5 -> x6, starting transfers between devices: 18.6 us -> 33.2 us  [exchanged(): return lax.all_to_all(pieces, axes, split_axis=0, concat_axis=0, tiled=True)]
    ppermute x0 -> x1, starting transfers between devices: none -> 8.73 us  [local(): other_half = lax.ppermute(own_half, 'core', [(0, 1), (1, 0)])]
    all_to_all x5 -> x6, waiting for transfers between devices: 34.1 us -> 28.5 us  [exchanged(): return lax.all_to_all(pieces, axes, split_axis=0, concat_axis=0, tiled=True)]
    another operation x0 -> x2, other arithmetic: none -> 2.53 us  [the longest x1 1.42 us: local(): jnp.stack([basis.reshape(-1, z_hi, half // z_hi) for basis in (own_half,...]
  transfers between devices with their start and end apart: 7 -> 9, of which waited for: 5 -> 6; matrix products, arithmetic and copies ran while one was open for 6% -> 7% of each run, Pallas kernels for 0% -> 0%
where the time goes in v5:
time: 187 us; the launch traced here: 186 us
  waiting for transfers between devices  81.3 us (43%)
  starting transfers between devices  42 us (22%)
  blocking collectives  24.6 us (13%)
  between operations  14.9 us (8%)
  local copies, waits for them, and re-layouts  9.86 us (5%)
  other arithmetic  6.84 us (4%)
  matrix products  6.17 us (3%)
    reduce_scatter x1, waiting for transfers between devices, local(): summed = lax.psum_scatter(partial, 'z_hi', scatter_dimension=0, tiled=True)  51.6 us
    all_to_all x6, starting transfers between devices, exchanged(): return lax.all_to_all(pieces, axes, split_axis=0, concat_axis=0, tiled=True)  33.2 us
    all_to_all x6, waiting for transfers between devices, exchanged(): return lax.all_to_all(pieces, axes, split_axis=0, concat_axis=0, tiled=True)  28.5 us
    all_to_all x2, blocking collectives, exchanged(): return lax.all_to_all(pieces, axes, split_axis=0, concat_axis=0, tiled=True)  24.6 us
    ppermute x1, starting transfers between devices, local(): other_half = lax.ppermute(own_half, 'core', [(0, 1), (1, 0)])  8.73 us
  transfers between devices with their start and end apart: 9, of which 6 were waited for; matrix products, arithmetic and copies ran while one was open for 7% of the time, Pallas kernels for 0%

profile of v5, /device:TPU:1, one launch (start us, length us, event | category | flops | bytes accessed | tf_op | source)
XLA Modules:
  0.0 185.7 jit_solution(12995710510420752549)
XLA Ops:
  7.2 1.2 copy.49
  8.5 1.0 broadcast_in_dim.9
  9.5 4.7 %all-to-all-start = ((bf16[4,256,512]{1,2,0:T(8,128)(2,1)}), bf16[4,256,512]{1,2,0:T(8,128)(2,1)S(1)}, u32[]{:S(2)}, u32[]{:S(2)}) async-start(bf16[4,256,512]{1,2,0:T(8,128)(2,1)} %broadcast_in_dim.9), calls=%async_computation | async-start | bytes 2097152 | tf_op jit(solution)/shard_map/all_to_all | solution.py:24
  14.7 1.1 pad.8
  15.8 6.7 %all-to-all-done = bf16[4,256,512]{1,2,0:T(8,128)(2,1)S(1)} async-done(((bf16[4,256,512]{1,2,0:T(8,128)(2,1)}), bf16[4,256,512]{1,2,0:T(8,128)(2,1)S(1)}, u32[]{:S(2)}, u32[]{:S(2)}) %all-to-all-start) | async-done | bytes 1048608 | tf_op jit(solution)/shard_map/all_to_all | solution.py:24
  22.6 3.5 %all-to-all-start.1 = ((bf16[4,256,512]{1,2,0:T(8,128)(2,1)}), bf16[4,256,512]{1,2,0:T(8,128)(2,1)S(1)}, u32[]{:S(2)}, u32[]{:S(2)}) async-start(bf16[4,256,512]{1,2,0:T(8,128)(2,1)} %bitcast.4), calls=%async_computation.1 | async-start | bytes 2097152 | tf_op jit(solution)/shard_map/all_to_all | solution.py:24
  26.2 8.7 %collective-permute-start = (bf16[1024,512]{0,1:T(8,128)(2,1)S(1)}, bf16[1024,512]{0,1:T(8,128)(2,1)}, u32[]{:S(2)}, u32[]{:S(2)}) collective-permute-start(bf16[1024,512]{0,1:T(8,128)(2,1)S(1)} %bitcast.55), channel_id=1, source_target_pairs={{0,1},{1,0},{2,3},{3,2},{4,5},{5,4},{6,7},{7,6},{8,9},{9,8},{10,11... | collective-permute-start | bytes 3145736 | tf_op jit(solution)/shard_map/ppermute | solution.py:73
  36.2 1.1 collective-permute-done
  37.3 1.9 %convolution_convert_fusion = bf16[512,512]{1,0:T(8,128)(2,1)S(1)} fusion(bf16[1024,512]{0,1:T(8,128)(2,1)} %collective-permute-done, bf16[1024,512]{1,0:T(8,128)(2,1)S(1)} %bitcast.66), kind=kOutput, calls=%fused_computation.2 | convolution fusion | flops 537133056 | bytes 2621440 | tf_op jit(solution)/shard_map/dot_general | solution.py:76
  39.3 1.1 pad_maximum_fusion.1
  41.9 3.8 %all-to-all-start.2 = ((f32[4,64,512]{2,1,0:T(8,128)}), f32[4,64,512]{2,1,0:T(8,128)S(1)}, u32[]{:S(2)}, u32[]{:S(2)}) async-start(f32[4,64,512]{2,1,0:T(8,128)} %copy.57), calls=%async_computation.3 | async-start | bytes 1048576 | tf_op jit(solution)/shard_map/all_to_all | solution.py:24
  45.7 1.4 pad_maximum_fusion
  47.3 3.9 %all-to-all-done.2 = f32[4,64,512]{2,1,0:T(8,128)S(1)} async-done(((f32[4,64,512]{2,1,0:T(8,128)}), f32[4,64,512]{2,1,0:T(8,128)S(1)}, u32[]{:S(2)}, u32[]{:S(2)}) %all-to-all-start.2) | async-done | bytes 524320 | tf_op jit(solution)/shard_map/all_to_all | solution.py:24
  51.3 51.6 %reduce-scatter.2.cloned.1.call-done = bf16[1,128,512]{2,1,0:T(8,128)(2,1)} async-done(((bf16[8,128,512]{2,1,0:T(8,128)(2,1)}), bf16[1,128,512]{2,1,0:T(8,128)(2,1)}) %reduce-scatter.2.cloned.1.call-update) | async-done | bytes 131088 | tf_op jit(solution)/shard_map/reduce_scatter | solution.py:86
  102.9 2.4 %multiply_reduce_fusion = (f32[]{:T(128)}, bf16[128,512]{1,0:T(8,128)(2,1)}) fusion(f32[2,128,512]{2,1,0:T(8,128)S(1)} %bitcast.61, bf16[1,128,512]{2,1,0:T(8,128)(2,1)} %reduce-scatter.2.cloned.1.call-done), kind=kLoop, calls=%fused_computation.19 | loop fusion | flops 983039 | bytes 786436 | tf_op jit(solution)/shard_map/reduce_sum | solution.py:102
  105.9 6.1 %all_to_all.40 = f32[4,8,128]{2,1,0:T(8,128)S(1)} all-to-all(f32[4,8,128]{2,1,0:T(8,128)S(1)} %broadcast_in_dim_broadcast_in_dim.3), channel_id=1, replica_groups=mesh['x_lo'=2,'z_hi'=8,'z_lo'=2,'y'=4,'x_hi'=2,'core'=2] {'x_lo','z_lo'}, dimensions={0} | all-to-all | bytes 32768 | tf_op jit(solution)/shard_map/all_to_all | solution.py:24
  112.0 18.6 %all_to_all.41 = f32[8,8,128]{2,1,0:T(8,128)S(1)} all-to-all(f32[8,8,128]{2,1,0:T(8,128)S(1)} %broadcast_in_dim.10), channel_id=1, replica_groups=mesh['x_lo'=2,'z_hi'=8,'z_lo'=2,'y'=4,'x_hi'=2,'core'=2] {'z_hi'}, dimensions={0} | all-to-all | bytes 65536 | tf_op jit(solution)/shard_map/all_to_all | solution.py:24
  131.2 14.3 %all-to-all-start.5 = ((f32[16,8,128]{2,1,0:T(8,128)}), f32[16,8,128]{2,1,0:T(8,128)S(1)}, u32[]{:S(2)}, u32[]{:S(2)}) async-start(f32[16,8,128]{2,1,0:T(8,128)} %broadcast_in_dim.11), calls=%async_computation.6 | async-start | bytes 131072 | tf_op jit(solution)/shard_map/all_to_all | solution.py:24
  145.5 1.0 fusion.9
  147.2 5.6 %all-to-all-done.5 = f32[16,8,128]{2,1,0:T(8,128)S(1)} async-done(((f32[16,8,128]{2,1,0:T(8,128)}), f32[16,8,128]{2,1,0:T(8,128)S(1)}, u32[]{:S(2)}, u32[]{:S(2)}) %all-to-all-start.5) | async-done | bytes 65568 | tf_op jit(solution)/shard_map/all_to_all | solution.py:24
  152.8 3.3 %all-to-all-start.7 = ((bf16[4,32,512]{2,1,0:T(8,128)(2,1)}), bf16[4,32,512]{2,1,0:T(8,128)(2,1)S(1)}, u32[]{:S(2)}, u32[]{:S(2)}) async-start(bf16[4,32,512]{2,1,0:T(8,128)(2,1)} %bitcast.27), calls=%async_computation.8 | async-start | bytes 262144 | tf_op jit(solution)/shard_map/all_to_all | solution.py:24
  157.4 3.5 %multiply_convert_fusion = bf16[1024,512]{1,0:T(8,128)(2,1)} fusion(bf16[1024,1024]{0,1:T(8,128)(2,1)S(1)} %bitcast.59, bf16[1024,512]{1,0:T(8,128)(2,1)} %all-gather.2.cloned.1.call-done, f32[]{:T(128)} %bitcast.22), kind=kOutput, calls=%fused_computation.1 | convolution fusion | flops 1074790400 | bytes 4194308 | tf_op jit(solution)/shard_map/dot_general | solution.py:111
  161.0 3.6 %all-to-all-start.6 = ((bf16[4,256,512]{2,1,0:T(8,128)(2,1)}), bf16[4,256,512]{2,1,0:T(8,128)(2,1)S(1)}, u32[]{:S(2)}, u32[]{:S(2)}) async-start(bf16[4,256,512]{2,1,0:T(8,128)(2,1)} %bitcast.23), calls=%async_computation.7 | async-start | bytes 2097152 | tf_op jit(solution)/shard_map/all_to_all | solution.py:24
  165.4 12.3 %all-to-all-done.6 = bf16[4,256,512]{2,1,0:T(8,128)(2,1)S(1)} async-done(((bf16[4,256,512]{2,1,0:T(8,128)(2,1)}), bf16[4,256,512]{2,1,0:T(8,128)(2,1)S(1)}, u32[]{:S(2)}, u32[]{:S(2)}) %all-to-all-start.6) | async-done | bytes 1048608 | tf_op jit(solution)/shard_map/all_to_all | solution.py:24
  (37 shorter events, 8.2 us)
Async XLA Ops:
  8.5 5.7 %copy-start = (bf16[256,1792]{1,0:T(8,128)(2,1)S(1)}, bf16[256,1792]{1,0:T(8,128)(2,1)}, u32[]{:S(2)}) copy-start(bf16[256,1792]{1,0:T(8,128)(2,1)} %param.4) | copy-start | bytes 2752516
  9.5 12.9 %all-to-all-start = ((bf16[4,256,512]{1,2,0:T(8,128)(2,1)}), bf16[4,256,512]{1,2,0:T(8,128)(2,1)S(1)}, u32[]{:S(2)}, u32[]{:S(2)}) async-start(bf16[4,256,512]{1,2,0:T(8,128)(2,1)} %broadcast_in_dim.9), calls=%async_computation | async-start | bytes 2097152 | tf_op jit(solution)/shard_map/all_to_all | solution.py:24
  22.6 12.3 %all-to-all-start.1 = ((bf16[4,256,512]{1,2,0:T(8,128)(2,1)}), bf16[4,256,512]{1,2,0:T(8,128)(2,1)S(1)}, u32[]{:S(2)}, u32[]{:S(2)}) async-start(bf16[4,256,512]{1,2,0:T(8,128)(2,1)} %bitcast.4), calls=%async_computation.1 | async-start | bytes 2097152 | tf_op jit(solution)/shard_map/all_to_all | solution.py:24
  26.1 76.7 %reduce-scatter.2.cloned.1.call-start = ((), (), s32[]{:S(2)}) async-start(), calls=%async_computation.9 | async-start | bytes 1179648 | tf_op jit(solution)/shard_map/reduce_scatter | solution.py:86
  26.2 11.1 %collective-permute-start = (bf16[1024,512]{0,1:T(8,128)(2,1)S(1)}, bf16[1024,512]{0,1:T(8,128)(2,1)}, u32[]{:S(2)}, u32[]{:S(2)}) collective-permute-start(bf16[1024,512]{0,1:T(8,128)(2,1)S(1)} %bitcast.55), channel_id=1, source_target_pairs={{0,1},{1,0},{2,3},{3,2},{4,5},{5,4},{6,7},{7,6},{8,9},{9,8},{10,11... | collective-permute-start | bytes 3145736 | tf_op jit(solution)/shard_map/ppermute | solution.py:73
  39.3 1.2 copy-start.1
  39.3 1.3 copy-start.2
  41.9 9.3 %all-to-all-start.2 = ((f32[4,64,512]{2,1,0:T(8,128)}), f32[4,64,512]{2,1,0:T(8,128)S(1)}, u32[]{:S(2)}, u32[]{:S(2)}) async-start(f32[4,64,512]{2,1,0:T(8,128)} %copy.57), calls=%async_computation.3 | async-start | bytes 1048576 | tf_op jit(solution)/shard_map/all_to_all | solution.py:24
  45.7 111.7 %all-gather.2.cloned.1.call-start = ((), (), s32[]{:S(2)}) async-start(), calls=%async_computation.10 | async-start | bytes 1179648 | tf_op jit(solution)/shard_map/all_gather | solution.py:101
  131.2 21.6 %all-to-all-start.5 = ((f32[16,8,128]{2,1,0:T(8,128)}), f32[16,8,128]{2,1,0:T(8,128)S(1)}, u32[]{:S(2)}, u32[]{:S(2)}) async-start(f32[16,8,128]{2,1,0:T(8,128)} %broadcast_in_dim.11), calls=%async_computation.6 | async-start | bytes 131072 | tf_op jit(solution)/shard_map/all_to_all | solution.py:24
  152.8 8.1 %all-to-all-start.7 = ((bf16[4,32,512]{2,1,0:T(8,128)(2,1)}), bf16[4,32,512]{2,1,0:T(8,128)(2,1)S(1)}, u32[]{:S(2)}, u32[]{:S(2)}) async-start(bf16[4,32,512]{2,1,0:T(8,128)(2,1)} %bitcast.27), calls=%async_computation.8 | async-start | bytes 262144 | tf_op jit(solution)/shard_map/all_to_all | solution.py:24
  161.0 16.8 %all-to-all-start.6 = ((bf16[4,256,512]{2,1,0:T(8,128)(2,1)}), bf16[4,256,512]{2,1,0:T(8,128)(2,1)S(1)}, u32[]{:S(2)}, u32[]{:S(2)}) async-start(bf16[4,256,512]{2,1,0:T(8,128)(2,1)} %bitcast.23), calls=%async_computation.7 | async-start | bytes 2097152 | tf_op jit(solution)/shard_map/all_to_all | solution.py:24
Sparse Core Ops, SparseCore 0:
  40.5 62.2 reduce-scatter.1
  105.5 48.8 all-gather.1

commit v6 on v5

--- a/solution.py
+++ b/solution.py
@@ -58,7 +58,7 @@
     rows = first_moment.shape[0]
     square = lax.axis_size(SQUARE)
     x_lo, z_hi, z_lo = (lax.axis_size(a) for a in ROW)
-    width = -(-columns // (square * LANES)) * LANES
+    width = columns // square
     half = ranks // 2
     core = lax.axis_index("core")
 
@@ -96,9 +96,10 @@
 
     summed = summed.reshape(square * rows, width)
     direction = adam(summed.astype(jnp.float32), moments[0], moments[1])[2]
-    step = direction.astype(jnp.bfloat16)
-    step, summed = lax.optimization_barrier((step, summed))
+    step = jnp.pad(direction.astype(jnp.bfloat16), ((0, 0), (0, -width % LANES)))
+    step, summed, moments = lax.optimization_barrier((step, summed, moments))
     step = lax.all_gather(step, "z_hi", axis=0, tiled=True)
+    direction = adam(summed.astype(jnp.float32), moments[0], moments[1])[2]
     total = summed_everywhere(jnp.sum(direction * direction))
 
     lowrank = own_first(summed.reshape(z_lo, x_lo, rows, width), 0).swapaxes(0, 1)
@@ -108,7 +109,7 @@
 
     root_mean = jnp.sqrt(total / (R * FF) + 1e-06)
     factor = jnp.minimum(1.0, clip_limit / root_mean)
-    projected = jnp.dot(whole, step, preferred_element_type=jnp.float32)
+    projected = jnp.dot(whole, step[:, :width], preferred_element_type=jnp.float32)
     updates = (factor * projected).astype(jnp.bfloat16)
     updates = exchanged(updates.reshape(square, block_rows, width), SQUARE)
     return (side_by_side(updates, columns), first_new, second_new)

time: 187 us -> 185 us (0.989)
  local copies, waits for them, and re-layouts: 9.86 us -> 14.1 us
  other arithmetic: 6.84 us -> 4.17 us
    unnamed x8 -> x13, local copies, waits for them, and re-layouts: 1.88 us -> 4.05 us
where the time goes in v6:
time: 185 us; the launch traced here: 184 us
  waiting for transfers between devices  81.1 us (44%)
  starting transfers between devices  41.3 us (22%)
  blocking collectives  24 us (13%)
  between operations  15 us (8%)
  local copies, waits for them, and re-layouts  14.1 us (8%)
  matrix products  4.51 us (2%)
  other arithmetic  4.17 us (2%)
    reduce_scatter x1, waiting for transfers between devices, local(): summed = lax.psum_scatter(partial, 'z_hi', scatter_dimension=0, tiled=True)  51.1 us
    all_to_all x6, starting transfers between devices, exchanged(): return lax.all_to_all(pieces, axes, split_axis=0, concat_axis=0, tiled=True)  32.5 us
    all_to_all x6, waiting for transfers between devices, exchanged(): return lax.all_to_all(pieces, axes, split_axis=0, concat_axis=0, tiled=True)  29.2 us
    all_to_all x2, blocking collectives, exchanged(): return lax.all_to_all(pieces, axes, split_axis=0, concat_axis=0, tiled=True)  24 us
    ppermute x1, starting transfers between devices, local(): other_half = lax.ppermute(own_half, 'core', [(0, 1), (1, 0)])  8.73 us
    unnamed x13, local copies, waits for them, and re-layouts  4.05 us
  transfers between devices with their start and end apart: 9, of which 6 were waited for; matrix products, arithmetic and copies ran while one was open for 7% of the time, Pallas kernels for 0%

profile of v6, /device:TPU:1, one launch (start us, length us, event | category | flops | bytes accessed | tf_op | source)
XLA Modules:
  0.0 184.0 jit_solution(14444738119917476894)
XLA Ops:
  7.2 1.2 copy.59
  8.5 1.0 broadcast_in_dim.9
  9.6 4.7 %all-to-all-start = ((bf16[4,256,512]{1,2,0:T(8,128)(2,1)}), bf16[4,256,512]{1,2,0:T(8,128)(2,1)S(1)}, u32[]{:S(2)}, u32[]{:S(2)}) async-start(bf16[4,256,512]{1,2,0:T(8,128)(2,1)} %broadcast_in_dim.9), calls=%async_computation | async-start | bytes 2097152 | tf_op jit(solution)/shard_map/all_to_all | solution.py:24
  14.2 1.3 copy.62
  15.5 7.0 %all-to-all-done = bf16[4,256,512]{1,2,0:T(8,128)(2,1)S(1)} async-done(((bf16[4,256,512]{1,2,0:T(8,128)(2,1)}), bf16[4,256,512]{1,2,0:T(8,128)(2,1)S(1)}, u32[]{:S(2)}, u32[]{:S(2)}) %all-to-all-start) | async-done | bytes 1048608 | tf_op jit(solution)/shard_map/all_to_all | solution.py:24
  22.6 3.5 %all-to-all-start.1 = ((bf16[4,256,448]{1,2,0:T(8,128)(2,1)}), bf16[4,256,448]{1,2,0:T(8,128)(2,1)S(1)}, u32[]{:S(2)}, u32[]{:S(2)}) async-start(bf16[4,256,448]{1,2,0:T(8,128)(2,1)} %bitcast.4), calls=%async_computation.1 | async-start | bytes 1835008 | tf_op jit(solution)/shard_map/all_to_all | solution.py:24
  26.2 8.7 %collective-permute-start = (bf16[1024,512]{0,1:T(8,128)(2,1)S(1)}, bf16[1024,512]{0,1:T(8,128)(2,1)S(1)}, u32[]{:S(2)}, u32[]{:S(2)}) collective-permute-start(bf16[1024,512]{0,1:T(8,128)(2,1)S(1)} %bitcast.63), channel_id=1, source_target_pairs={{0,1},{1,0},{2,3},{3,2},{4,5},{5,4},{6,7},{7,6},{8,9},{9,8},{10,11... | collective-permute-start | bytes 3145736 | tf_op jit(solution)/shard_map/ppermute | solution.py:73
  35.1 1.5 convolution_convert_fusion.1
  38.1 1.2 copy.64
  39.5 1.1 copy.66
  42.2 3.8 %all-to-all-start.2 = ((f32[4,64,448]{2,1,0:T(8,128)}), f32[4,64,448]{2,1,0:T(8,128)S(1)}, u32[]{:S(2)}, u32[]{:S(2)}) async-start(f32[4,64,448]{2,1,0:T(8,128)} %copy.68), calls=%async_computation.3 | async-start | bytes 1048576 | tf_op jit(solution)/shard_map/all_to_all | solution.py:24
  46.4 5.1 %all-to-all-done.2 = f32[4,64,448]{2,1,0:T(8,128)S(1)} async-done(((f32[4,64,448]{2,1,0:T(8,128)}), f32[4,64,448]{2,1,0:T(8,128)S(1)}, u32[]{:S(2)}, u32[]{:S(2)}) %all-to-all-start.2) | async-done | bytes 458784 | tf_op jit(solution)/shard_map/all_to_all | solution.py:24
  51.6 51.1 %reduce-scatter.2.cloned.1.call-done = bf16[1,128,448]{2,1,0:T(8,128)(2,1)} async-done(((bf16[8,128,448]{2,1,0:T(8,128)(2,1)}), bf16[1,128,448]{2,1,0:T(8,128)(2,1)}) %reduce-scatter.2.cloned.1.call-update) | async-done | bytes 114704 | tf_op jit(solution)/shard_map/reduce_scatter | solution.py:86
  102.7 1.2 fusion.16
  104.6 1.7 fusion.17
  106.9 5.9 %all_to_all.40 = f32[4,8,128]{2,1,0:T(8,128)S(1)} all-to-all(f32[4,8,128]{2,1,0:T(8,128)S(1)} %broadcast_in_dim_broadcast_in_dim.3), channel_id=1, replica_groups=mesh['x_lo'=2,'z_hi'=8,'z_lo'=2,'y'=4,'x_hi'=2,'core'=2] {'x_lo','z_lo'}, dimensions={0} | all-to-all | bytes 32768 | tf_op jit(solution)/shard_map/all_to_all | solution.py:24
  112.9 18.1 %all_to_all.41 = f32[8,8,128]{2,1,0:T(8,128)S(1)} all-to-all(f32[8,8,128]{2,1,0:T(8,128)S(1)} %broadcast_in_dim.10), channel_id=1, replica_groups=mesh['x_lo'=2,'z_hi'=8,'z_lo'=2,'y'=4,'x_hi'=2,'core'=2] {'z_hi'}, dimensions={0} | all-to-all | bytes 65536 | tf_op jit(solution)/shard_map/all_to_all | solution.py:24
  131.6 13.6 %all-to-all-start.5 = ((f32[16,8,128]{2,1,0:T(8,128)}), f32[16,8,128]{2,1,0:T(8,128)S(1)}, u32[]{:S(2)}, u32[]{:S(2)}) async-start(f32[16,8,128]{2,1,0:T(8,128)} %broadcast_in_dim.11), calls=%async_computation.6 | async-start | bytes 131072 | tf_op jit(solution)/shard_map/all_to_all | solution.py:24
  145.9 6.6 %all-to-all-done.5 = f32[16,8,128]{2,1,0:T(8,128)S(1)} async-done(((f32[16,8,128]{2,1,0:T(8,128)}), f32[16,8,128]{2,1,0:T(8,128)S(1)}, u32[]{:S(2)}, u32[]{:S(2)}) %all-to-all-start.5) | async-done | bytes 65568 | tf_op jit(solution)/shard_map/all_to_all | solution.py:24
  152.5 3.3 %all-to-all-start.7 = ((bf16[4,32,448]{2,1,0:T(8,128)(2,1)}), bf16[4,32,448]{2,1,0:T(8,128)(2,1)S(1)}, u32[]{:S(2)}, u32[]{:S(2)}) async-start(bf16[4,32,448]{2,1,0:T(8,128)(2,1)} %bitcast.26), calls=%async_computation.8 | async-start | bytes 262144 | tf_op jit(solution)/shard_map/all_to_all | solution.py:24
  157.1 2.4 %multiply_convert_fusion = bf16[1024,448]{0,1:T(8,128)(2,1)S(1)} fusion(bf16[1024,1024]{0,1:T(8,128)(2,1)S(1)} %bitcast.68, bf16[1024,512]{1,0:T(8,128)(2,1)} %all-gather.2.cloned.1.call-done, f32[]{:T(128)} %bitcast.21), kind=kOutput, calls=%fused_computation.1 | convolution fusion | flops 940441600 | bytes 4063236 | tf_op jit(solution)/shard_map/dot_general | solution.py:112
  160.5 3.6 %all-to-all-start.6 = ((bf16[4,256,448]{1,2,0:T(8,128)(2,1)}), bf16[4,256,448]{1,2,0:T(8,128)(2,1)S(1)}, u32[]{:S(2)}, u32[]{:S(2)}) async-start(bf16[4,256,448]{1,2,0:T(8,128)(2,1)} %bitcast.58), calls=%async_computation.7 | async-start | bytes 1835008 | tf_op jit(solution)/shard_map/all_to_all | solution.py:24
  165.4 10.5 %all-to-all-done.6 = bf16[4,256,448]{1,2,0:T(8,128)(2,1)S(1)} async-done(((bf16[4,256,448]{1,2,0:T(8,128)(2,1)}), bf16[4,256,448]{1,2,0:T(8,128)(2,1)S(1)}, u32[]{:S(2)}, u32[]{:S(2)}) %all-to-all-start.6) | async-done | bytes 917536 | tf_op jit(solution)/shard_map/all_to_all | solution.py:24
  175.8 1.4 copy.73
  (47 shorter events, 9.6 us)
Async XLA Ops:
  8.5 5.7 %copy-start.1 = (bf16[256,1792]{1,0:T(8,128)(2,1)S(1)}, bf16[256,1792]{1,0:T(8,128)(2,1)}, u32[]{:S(2)}) copy-start(bf16[256,1792]{1,0:T(8,128)(2,1)} %param.4) | copy-start | bytes 2752516
  9.6 12.9 %all-to-all-start = ((bf16[4,256,512]{1,2,0:T(8,128)(2,1)}), bf16[4,256,512]{1,2,0:T(8,128)(2,1)S(1)}, u32[]{:S(2)}, u32[]{:S(2)}) async-start(bf16[4,256,512]{1,2,0:T(8,128)(2,1)} %broadcast_in_dim.9), calls=%async_computation | async-start | bytes 2097152 | tf_op jit(solution)/shard_map/all_to_all | solution.py:24
  22.6 12.3 %all-to-all-start.1 = ((bf16[4,256,448]{1,2,0:T(8,128)(2,1)}), bf16[4,256,448]{1,2,0:T(8,128)(2,1)S(1)}, u32[]{:S(2)}, u32[]{:S(2)}) async-start(bf16[4,256,448]{1,2,0:T(8,128)(2,1)} %bitcast.4), calls=%async_computation.1 | async-start | bytes 1835008 | tf_op jit(solution)/shard_map/all_to_all | solution.py:24
  26.1 76.6 %reduce-scatter.2.cloned.1.call-start = ((), (), s32[]{:S(2)}) async-start(), calls=%async_computation.9 | async-start | bytes 1179648 | tf_op jit(solution)/shard_map/reduce_scatter | solution.py:86
  26.2 11.0 %collective-permute-start = (bf16[1024,512]{0,1:T(8,128)(2,1)S(1)}, bf16[1024,512]{0,1:T(8,128)(2,1)S(1)}, u32[]{:S(2)}, u32[]{:S(2)}) collective-permute-start(bf16[1024,512]{0,1:T(8,128)(2,1)S(1)} %bitcast.63), channel_id=1, source_target_pairs={{0,1},{1,0},{2,3},{3,2},{4,5},{5,4},{6,7},{7,6},{8,9},{9,8},{10,11... | collective-permute-start | bytes 3145736 | tf_op jit(solution)/shard_map/ppermute | solution.py:73
  39.5 1.1 copy-start.2
  39.5 1.3 copy-start.3
  42.2 9.3 %all-to-all-start.2 = ((f32[4,64,448]{2,1,0:T(8,128)}), f32[4,64,448]{2,1,0:T(8,128)S(1)}, u32[]{:S(2)}, u32[]{:S(2)}) async-start(f32[4,64,448]{2,1,0:T(8,128)} %copy.68), calls=%async_computation.3 | async-start | bytes 1048576 | tf_op jit(solution)/shard_map/all_to_all | solution.py:24
  46.0 111.1 %all-gather.2.cloned.1.call-start = ((), (), s32[]{:S(2)}) async-start(), calls=%async_computation.10 | async-start | bytes 1179648 | tf_op jit(solution)/shard_map/all_gather | solution.py:101
  102.7 42.5 %copy-start = (bf16[1,128,448]{2,1,0:T(8,128)(2,1)S(1)}, bf16[1,128,448]{2,1,0:T(8,128)(2,1)}, u32[]{:S(2)}) copy-start(bf16[1,128,448]{2,1,0:T(8,128)(2,1)} %reduce-scatter.2.cloned.1.call-done) | copy-start | bytes 344068
  131.6 20.9 %all-to-all-start.5 = ((f32[16,8,128]{2,1,0:T(8,128)}), f32[16,8,128]{2,1,0:T(8,128)S(1)}, u32[]{:S(2)}, u32[]{:S(2)}) async-start(f32[16,8,128]{2,1,0:T(8,128)} %broadcast_in_dim.11), calls=%async_computation.6 | async-start | bytes 131072 | tf_op jit(solution)/shard_map/all_to_all | solution.py:24
  152.5 8.0 %all-to-all-start.7 = ((bf16[4,32,448]{2,1,0:T(8,128)(2,1)}), bf16[4,32,448]{2,1,0:T(8,128)(2,1)S(1)}, u32[]{:S(2)}, u32[]{:S(2)}) async-start(bf16[4,32,448]{2,1,0:T(8,128)(2,1)} %bitcast.26), calls=%async_computation.8 | async-start | bytes 262144 | tf_op jit(solution)/shard_map/all_to_all | solution.py:24
  159.5 5.1 %copy-start.4 = (f32[32,1792]{1,0:T(8,128)S(1)}, f32[32,1792]{1,0:T(8,128)}, u32[]{:S(2)}) copy-start(f32[32,1792]{1,0:T(8,128)} %param.6) | copy-start | bytes 688132
  160.5 15.3 %all-to-all-start.6 = ((bf16[4,256,448]{1,2,0:T(8,128)(2,1)}), bf16[4,256,448]{1,2,0:T(8,128)(2,1)S(1)}, u32[]{:S(2)}, u32[]{:S(2)}) async-start(bf16[4,256,448]{1,2,0:T(8,128)(2,1)} %bitcast.58), calls=%async_computation.7 | async-start | bytes 1835008 | tf_op jit(solution)/shard_map/all_to_all | solution.py:24
Sparse Core Ops, SparseCore 0:
  40.7 61.9 reduce-scatter.1
  105.4 49.2 all-gather.1

commit v7 on v6

--- a/solution.py
+++ b/solution.py
@@ -1,6 +1,7 @@
 import jax
 import jax.numpy as jnp
 from jax import lax
+from jax.experimental import pallas as pl
 from jax.sharding import Mesh
 from jax.sharding import PartitionSpec as P
 
@@ -45,6 +46,38 @@
     return first_new, second_new, direction
 
 
+def projected_sums(own_half, other_half, block, square, groups):
+    depth, half = own_half.shape
+    width = block.shape[1]
+    count = half // groups
+
+    def kernel(own_ref, other_ref, block_ref, out_ref):
+        for place, ref in enumerate((own_ref, other_ref)):
+            total = jnp.zeros((half, width), jnp.float32)
+            for k in range(square):
+                total += lax.dot_general(
+                    ref[k], block_ref[k], (((1,), (1,)), ((), ())), preferred_element_type=jnp.float32
+                )
+            total = total.astype(jnp.bfloat16)
+            for group in range(groups):
+                out_ref[group, place * count : (place + 1) * count, :] = total[
+                    group * count : (group + 1) * count, :
+                ]
+
+    def turned(array):
+        return array.reshape(square, depth // square, -1).swapaxes(1, 2)
+
+    return pl.pallas_call(
+        kernel,
+        out_shape=jax.ShapeDtypeStruct((groups, 2 * count, width), jnp.bfloat16),
+        cost_estimate=pl.CostEstimate(
+            flops=4 * depth * half * width,
+            bytes_accessed=4 * depth * half + 2 * depth * width + 4 * half * width,
+            transcendentals=0,
+        ),
+    )(turned(own_half), turned(other_half), turned(block))
+
+
 def summed_everywhere(value):
     value = jnp.full((8, LANES), value, jnp.float32)
     for axes in (SQUARE, "z_hi", COL):
@@ -72,14 +105,7 @@
     own_half, blocks = lax.optimization_barrier((own_half, blocks))
     other_half = lax.ppermute(own_half, "core", [(0, 1), (1, 0)])
     block = exchanged(blocks, SQUARE).reshape(square * block_rows, width)
-    partial = [
-        lax.dot_general(
-            basis, block, (((0,), (0,)), ((), ())), preferred_element_type=jnp.float32
-        ).astype(jnp.bfloat16)
-        for basis in (own_half, other_half)
-    ]
-    partial = jnp.stack([p.reshape(z_hi, half // z_hi, width) for p in partial], axis=1)
-    partial = partial.reshape(z_hi, ranks // z_hi, width)
+    partial = projected_sums(own_half, other_half, block, square, z_hi)
     partial, own_half, other_half, first_moment, second_moment = lax.optimization_barrier(
         (partial, own_half, other_half, first_moment, second_moment)
     )

time: 185 us -> 186 us (level)
  blocking collectives: 24 us -> 7.26 us
  starting transfers between devices: 41.3 us -> 48.7 us
  waiting for transfers between devices: 81.1 us -> 86 us
  Pallas kernels: 0 us -> 4.1 us
  matrix products: 4.51 us -> 2.38 us
    all_to_all x2 -> x1, blocking collectives: 24 us -> 7.26 us  [exchanged(): return lax.all_to_all(pieces, axes, split_axis=0, concat_axis=0, tiled=True)]
    all_to_all x6 -> x7, waiting for transfers between devices: 29.2 us -> 40.2 us  [exchanged(): return lax.all_to_all(pieces, axes, split_axis=0, concat_axis=0, tiled=True)]
    all_to_all x6 -> x7, starting transfers between devices: 32.5 us -> 39.9 us  [exchanged(): return lax.all_to_all(pieces, axes, split_axis=0, concat_axis=0, tiled=True)]
    reduce_scatter x1, waiting for transfers between devices: 51.1 us -> 44.8 us  [local(): summed = lax.psum_scatter(partial, 'z_hi', scatter_dimension=0, tiled=True)]
    pallas_call x0 -> x1, Pallas kernels: none -> 4.1 us  [projected_sums(): pl.pallas_call(kernel, out_shape=jax.ShapeDtypeStruct((groups, 2 * count,...]
    reshape x2 -> x3, local copies, waits for them, and re-layouts: 0.24 us -> 2.64 us  [the longest x2 2.63 us: turned(): return array.reshape(square, depth // square, -1).swapaxes(1, 2)]
    dot_general x2 -> x0, matrix products: 2.12 us -> none  [local(): lax.dot_general(basis, block, (((0,), (0,)), ((), ())), preferred_element...]
    select_n x1 -> x2, other arithmetic: 0.04 us -> 2 us  [own_first(): return jnp.where(core == 0, array, jnp.flip(array, axis))]
  transfers between devices with their start and end apart: 9 -> 10, of which waited for: 6 -> 7; matrix products, arithmetic and copies ran while one was open for 7% -> 10% of each run, Pallas kernels for 0% -> 0%
where the time goes in v7:
time: 186 us; the launch traced here: 185 us
  waiting for transfers between devices  86 us (46%)
  starting transfers between devices  48.7 us (26%)
  local copies, waits for them, and re-layouts  15.9 us (9%)
  between operations  15 us (8%)
  blocking collectives  7.26 us (4%)
  other arithmetic  5.98 us (3%)
  Pallas kernels  4.1 us (2%)
  matrix products  2.38 us (1%)
    reduce_scatter x1, waiting for transfers between devices, local(): summed = lax.psum_scatter(partial, 'z_hi', scatter_dimension=0, tiled=True)  44.8 us
    all_to_all x7, waiting for transfers between devices, exchanged(): return lax.all_to_all(pieces, axes, split_axis=0, concat_axis=0, tiled=True)  40.2 us
    all_to_all x7, starting transfers between devices, exchanged(): return lax.all_to_all(pieces, axes, split_axis=0, concat_axis=0, tiled=True)  39.9 us
    ppermute x1, starting transfers between devices, local(): other_half = lax.ppermute(own_half, 'core', [(0, 1), (1, 0)])  8.76 us
    all_to_all x1, blocking collectives, exchanged(): return lax.all_to_all(pieces, axes, split_axis=0, concat_axis=0, tiled=True)  7.26 us
    unnamed x15, local copies, waits for them, and re-layouts  4.84 us
    pallas_call x1, Pallas kernels, projected_sums(): pl.pallas_call(kernel, out_shape=jax.ShapeDtypeStruct((groups, 2 * count,...  4.1 us
  transfers between devices with their start and end apart: 10, of which 7 were waited for; matrix products, arithmetic and copies ran while one was open for 10% of the time, Pallas kernels for 0%

profile of v7, /device:TPU:1, one launch (start us, length us, event | category | flops | bytes accessed | tf_op | source)
XLA Modules:
  0.0 185.4 jit_solution(9518911563894843674)
XLA Ops:
  7.2 1.2 copy.55
  9.7 4.7 %all-to-all-start = ((bf16[4,256,512]{2,1,0:T(8,128)(2,1)}), bf16[4,256,512]{2,1,0:T(8,128)(2,1)S(1)}, u32[]{:S(2)}, u32[]{:S(2)}) async-start(bf16[4,256,512]{2,1,0:T(8,128)(2,1)} %broadcast_in_dim.9), calls=%async_computation | async-start | bytes 2097152 | tf_op jit(solution)/shard_map/all_to_all | solution.py:25
  14.4 1.3 copy.58
  15.6 7.0 %all-to-all-done = bf16[4,256,512]{2,1,0:T(8,128)(2,1)S(1)} async-done(((bf16[4,256,512]{2,1,0:T(8,128)(2,1)}), bf16[4,256,512]{2,1,0:T(8,128)(2,1)S(1)}, u32[]{:S(2)}, u32[]{:S(2)}) %all-to-all-start) | async-done | bytes 1048608 | tf_op jit(solution)/shard_map/all_to_all | solution.py:25
  22.6 3.5 %all-to-all-start.1 = ((bf16[4,256,448]{1,2,0:T(8,128)(2,1)}), bf16[4,256,448]{1,2,0:T(8,128)(2,1)S(1)}, u32[]{:S(2)}, u32[]{:S(2)}) async-start(bf16[4,256,448]{1,2,0:T(8,128)(2,1)} %bitcast.5), calls=%async_computation.1 | async-start | bytes 1835008 | tf_op jit(solution)/shard_map/all_to_all | solution.py:25
  26.2 8.8 %collective-permute-start = (bf16[1024,512]{1,0:T(8,128)(2,1)S(1)}, bf16[1024,512]{1,0:T(8,128)(2,1)S(1)}, u32[]{:S(2)}, u32[]{:S(2)}) collective-permute-start(bf16[1024,512]{1,0:T(8,128)(2,1)S(1)} %bitcast.54), channel_id=1, source_target_pairs={{0,1},{1,0},{2,3},{3,2},{4,5},{5,4},{6,7},{7,6},{8,9},{9,8},{10,11... | collective-permute-start | bytes 3145736 | tf_op jit(solution)/shard_map/ppermute | solution.py:106
  35.0 1.3 copy.59
  37.2 1.3 copy.60
  39.5 4.1 %shard_map.67 = bf16[8,128,448]{2,1,0:T(8,128)(2,1)} custom-call(bf16[4,512,256]{2,1,0:T(8,128)(2,1)} %bitcast.59, bf16[4,512,256]{2,1,0:T(8,128)(2,1)} %bitcast.60, bf16[4,448,256]{2,1,0:T(8,128)(2,1)} %bitcast.64), custom_call_target="tpu_custom_call" | custom-call | flops 939524096 | bytes 3932160 | tf_op jit(solution)/shard_map/pallas_call | solution.py:70
  45.1 4.1 %all-to-all-start.2 = ((f32[4,64,448]{2,1,0:T(8,128)}), f32[4,64,448]{2,1,0:T(8,128)}, u32[]{:S(2)}, u32[]{:S(2)}) async-start(f32[4,64,448]{2,1,0:T(8,128)} %copy.64), calls=%async_computation.3 | async-start | bytes 1048576 | tf_op jit(solution)/shard_map/all_to_all | solution.py:25
  50.8 4.2 %all-to-all-done.2 = f32[4,64,448]{2,1,0:T(8,128)} async-done(((f32[4,64,448]{2,1,0:T(8,128)}), f32[4,64,448]{2,1,0:T(8,128)}, u32[]{:S(2)}, u32[]{:S(2)}) %all-to-all-start.2) | async-done | bytes 458784 | tf_op jit(solution)/shard_map/all_to_all | solution.py:25
  55.0 1.3 reverse_select_fusion
  56.3 44.8 %reduce-scatter.2.cloned.1.call-done = bf16[1,128,448]{2,1,0:T(8,128)(2,1)} async-done(((bf16[8,128,448]{2,1,0:T(8,128)(2,1)}), bf16[1,128,448]{2,1,0:T(8,128)(2,1)}) %reduce-scatter.2.cloned.1.call-update) | async-done | bytes 114704 | tf_op jit(solution)/shard_map/reduce_scatter | solution.py:112
  103.0 1.7 fusion.17
  105.3 7.3 %all_to_all.40 = f32[4,8,128]{2,1,0:T(8,128)S(1)} all-to-all(f32[4,8,128]{2,1,0:T(8,128)S(1)} %broadcast_in_dim_broadcast_in_dim.3), channel_id=1, replica_groups=mesh['x_lo'=2,'z_hi'=8,'z_lo'=2,'y'=4,'x_hi'=2,'core'=2] {'x_lo','z_lo'}, dimensions={0} | all-to-all | bytes 32768 | tf_op jit(solution)/shard_map/all_to_all | solution.py:25
  113.2 6.6 %all-to-all-start.4 = ((f32[8,8,128]{2,1,0:T(8,128)}), f32[8,8,128]{2,1,0:T(8,128)S(1)}, u32[]{:S(2)}, u32[]{:S(2)}) async-start(f32[8,8,128]{2,1,0:T(8,128)} %broadcast_in_dim.10), calls=%async_computation.5 | async-start | bytes 65536 | tf_op jit(solution)/shard_map/all_to_all | solution.py:25
  119.9 11.9 %all-to-all-done.4 = f32[8,8,128]{2,1,0:T(8,128)S(1)} async-done(((f32[8,8,128]{2,1,0:T(8,128)}), f32[8,8,128]{2,1,0:T(8,128)S(1)}, u32[]{:S(2)}, u32[]{:S(2)}) %all-to-all-start.4) | async-done | bytes 32800 | tf_op jit(solution)/shard_map/all_to_all | solution.py:25
  132.4 14.0 %all-to-all-start.5 = ((f32[16,8,128]{2,1,0:T(8,128)}), f32[16,8,128]{2,1,0:T(8,128)S(1)}, u32[]{:S(2)}, u32[]{:S(2)}) async-start(f32[16,8,128]{2,1,0:T(8,128)} %broadcast_in_dim.11), calls=%async_computation.6 | async-start | bytes 131072 | tf_op jit(solution)/shard_map/all_to_all | solution.py:25
  147.2 6.6 %all-to-all-done.5 = f32[16,8,128]{2,1,0:T(8,128)S(1)} async-done(((f32[16,8,128]{2,1,0:T(8,128)}), f32[16,8,128]{2,1,0:T(8,128)S(1)}, u32[]{:S(2)}, u32[]{:S(2)}) %all-to-all-start.5) | async-done | bytes 65568 | tf_op jit(solution)/shard_map/all_to_all | solution.py:25
  153.8 3.3 %all-to-all-start.7 = ((bf16[4,32,448]{2,1,0:T(8,128)(2,1)}), bf16[4,32,448]{2,1,0:T(8,128)(2,1)S(1)}, u32[]{:S(2)}, u32[]{:S(2)}) async-start(bf16[4,32,448]{2,1,0:T(8,128)(2,1)} %bitcast.29), calls=%async_computation.8 | async-start | bytes 262144 | tf_op jit(solution)/shard_map/all_to_all | solution.py:25
  158.4 2.4 %multiply_convert_fusion = bf16[1024,448]{0,1:T(8,128)(2,1)S(1)} fusion(bf16[1024,1024]{0,1:T(8,128)(2,1)S(1)} %bitcast.65, bf16[1024,512]{1,0:T(8,128)(2,1)} %all-gather.2.cloned.1.call-done, f32[]{:T(128)} %bitcast.24), kind=kOutput, calls=%fused_computation.1 | convolution fusion | flops 940441600 | bytes 4063236 | tf_op jit(solution)/shard_map/dot_general | solution.py:138
  161.8 3.6 %all-to-all-start.6 = ((bf16[4,256,448]{1,2,0:T(8,128)(2,1)}), bf16[4,256,448]{1,2,0:T(8,128)(2,1)S(1)}, u32[]{:S(2)}, u32[]{:S(2)}) async-start(bf16[4,256,448]{1,2,0:T(8,128)(2,1)} %bitcast.53), calls=%async_computation.7 | async-start | bytes 1835008 | tf_op jit(solution)/shard_map/all_to_all | solution.py:25
  166.7 10.5 %all-to-all-done.6 = bf16[4,256,448]{1,2,0:T(8,128)(2,1)S(1)} async-done(((bf16[4,256,448]{1,2,0:T(8,128)(2,1)}), bf16[4,256,448]{1,2,0:T(8,128)(2,1)S(1)}, u32[]{:S(2)}, u32[]{:S(2)}) %all-to-all-start.6) | async-done | bytes 917536 | tf_op jit(solution)/shard_map/all_to_all | solution.py:25
  177.1 1.4 copy.70
  (48 shorter events, 13.5 us)
Async XLA Ops:
  8.5 5.9 %copy-start.2 = (bf16[256,1792]{1,0:T(8,128)(2,1)S(1)}, bf16[256,1792]{1,0:T(8,128)(2,1)}, u32[]{:S(2)}) copy-start(bf16[256,1792]{1,0:T(8,128)(2,1)} %param.4) | copy-start | bytes 2752516
  9.7 12.9 %all-to-all-start = ((bf16[4,256,512]{2,1,0:T(8,128)(2,1)}), bf16[4,256,512]{2,1,0:T(8,128)(2,1)S(1)}, u32[]{:S(2)}, u32[]{:S(2)}) async-start(bf16[4,256,512]{2,1,0:T(8,128)(2,1)} %broadcast_in_dim.9), calls=%async_computation | async-start | bytes 2097152 | tf_op jit(solution)/shard_map/all_to_all | solution.py:25
  22.6 15.9 %all-to-all-start.1 = ((bf16[4,256,448]{1,2,0:T(8,128)(2,1)}), bf16[4,256,448]{1,2,0:T(8,128)(2,1)S(1)}, u32[]{:S(2)}, u32[]{:S(2)}) async-start(bf16[4,256,448]{1,2,0:T(8,128)(2,1)} %bitcast.5), calls=%async_computation.1 | async-start | bytes 1835008 | tf_op jit(solution)/shard_map/all_to_all | solution.py:25
  26.2 75.0 %reduce-scatter.2.cloned.1.call-start = ((), (), s32[]{:S(2)}) async-start(), calls=%async_computation.9 | async-start | bytes 1179648 | tf_op jit(solution)/shard_map/reduce_scatter | solution.py:112
  26.2 11.0 %collective-permute-start = (bf16[1024,512]{1,0:T(8,128)(2,1)S(1)}, bf16[1024,512]{1,0:T(8,128)(2,1)S(1)}, u32[]{:S(2)}, u32[]{:S(2)}) collective-permute-start(bf16[1024,512]{1,0:T(8,128)(2,1)S(1)} %bitcast.54), channel_id=1, source_target_pairs={{0,1},{1,0},{2,3},{3,2},{4,5},{5,4},{6,7},{7,6},{8,9},{9,8},{10,11... | collective-permute-start | bytes 3145736 | tf_op jit(solution)/shard_map/ppermute | solution.py:106
  38.6 0.9 copy-start
  39.5 4.1 %copy-start.3 = (f32[32,1792]{1,0:T(8,128)S(1)}, f32[32,1792]{1,0:T(8,128)}, u32[]{:S(2)}) copy-start(f32[32,1792]{1,0:T(8,128)} %param.7) | copy-start | bytes 688132
  39.5 4.1 %copy-start.4 = (f32[32,1792]{1,0:T(8,128)S(1)}, f32[32,1792]{1,0:T(8,128)}, u32[]{:S(2)}) copy-start(f32[32,1792]{1,0:T(8,128)} %param.6) | copy-start | bytes 688132
  45.1 9.8 %all-to-all-start.2 = ((f32[4,64,448]{2,1,0:T(8,128)}), f32[4,64,448]{2,1,0:T(8,128)}, u32[]{:S(2)}, u32[]{:S(2)}) async-start(f32[4,64,448]{2,1,0:T(8,128)} %copy.64), calls=%async_computation.3 | async-start | bytes 1048576 | tf_op jit(solution)/shard_map/all_to_all | solution.py:25
  49.3 109.1 %all-gather.2.cloned.1.call-start = ((), (), s32[]{:S(2)}) async-start(), calls=%async_computation.10 | async-start | bytes 1179648 | tf_op jit(solution)/shard_map/all_gather | solution.py:127
  101.1 18.8 %copy-start.1 = (bf16[1,128,448]{2,1,0:T(8,128)(2,1)S(1)}, bf16[1,128,448]{2,1,0:T(8,128)(2,1)}, u32[]{:S(2)}) copy-start(bf16[1,128,448]{2,1,0:T(8,128)(2,1)} %reduce-scatter.2.cloned.1.call-done) | copy-start | bytes 344068
  113.2 18.6 %all-to-all-start.4 = ((f32[8,8,128]{2,1,0:T(8,128)}), f32[8,8,128]{2,1,0:T(8,128)S(1)}, u32[]{:S(2)}, u32[]{:S(2)}) async-start(f32[8,8,128]{2,1,0:T(8,128)} %broadcast_in_dim.10), calls=%async_computation.5 | async-start | bytes 65536 | tf_op jit(solution)/shard_map/all_to_all | solution.py:25
  132.4 21.4 %all-to-all-start.5 = ((f32[16,8,128]{2,1,0:T(8,128)}), f32[16,8,128]{2,1,0:T(8,128)S(1)}, u32[]{:S(2)}, u32[]{:S(2)}) async-start(f32[16,8,128]{2,1,0:T(8,128)} %broadcast_in_dim.11), calls=%async_computation.6 | async-start | bytes 131072 | tf_op jit(solution)/shard_map/all_to_all | solution.py:25
  153.8 8.0 %all-to-all-start.7 = ((bf16[4,32,448]{2,1,0:T(8,128)(2,1)}), bf16[4,32,448]{2,1,0:T(8,128)(2,1)S(1)}, u32[]{:S(2)}, u32[]{:S(2)}) async-start(bf16[4,32,448]{2,1,0:T(8,128)(2,1)} %bitcast.29), calls=%async_computation.8 | async-start | bytes 262144 | tf_op jit(solution)/shard_map/all_to_all | solution.py:25
  160.8 5.1 %copy-start.5 = (f32[32,1792]{1,0:T(8,128)S(1)}, f32[32,1792]{1,0:T(8,128)}, u32[]{:S(2)}) copy-start(f32[32,1792]{1,0:T(8,128)} %param.6) | copy-start | bytes 688132
  161.8 15.3 %all-to-all-start.6 = ((bf16[4,256,448]{1,2,0:T(8,128)(2,1)}), bf16[4,256,448]{1,2,0:T(8,128)(2,1)S(1)}, u32[]{:S(2)}, u32[]{:S(2)}) async-start(bf16[4,256,448]{1,2,0:T(8,128)(2,1)} %bitcast.53), calls=%async_computation.7 | async-start | bytes 1835008 | tf_op jit(solution)/shard_map/all_to_all | solution.py:25
Sparse Core Ops, SparseCore 0:
  43.7 57.3 reduce-scatter.1
  103.8 50.6 all-gather.1

commit v8 on v7

--- a/solution.py
+++ b/solution.py
@@ -2,6 +2,7 @@
 import jax.numpy as jnp
 from jax import lax
 from jax.experimental import pallas as pl
+from jax.experimental.pallas import tpu as pltpu
 from jax.sharding import Mesh
 from jax.sharding import PartitionSpec as P
 
@@ -69,6 +70,8 @@
 
     return pl.pallas_call(
         kernel,
+        in_specs=[pl.BlockSpec(memory_space=pltpu.VMEM)] * 3,
+        compiler_params=pltpu.CompilerParams(vmem_limit_bytes=24 * 1024 * 1024),
         out_shape=jax.ShapeDtypeStruct((groups, 2 * count, width), jnp.bfloat16),
         cost_estimate=pl.CostEstimate(
             flops=4 * depth * half * width,

time: 186 us -> 183 us (0.984)
  Pallas kernels: 4.1 us -> 2.23 us
    pallas_call x1, Pallas kernels: 4.1 us -> 2.23 us  [projected_sums(): pl.pallas_call(kernel, in_specs=[pl.BlockSpec(memory_space=pltpu.VMEM)] *...]
where the time goes in v8:
time: 183 us; the launch traced here: 182 us
  waiting for transfers between devices  86.7 us (47%)
  starting transfers between devices  47.7 us (26%)
  local copies, waits for them, and re-layouts  15.3 us (8%)
  between operations  15 us (8%)
  blocking collectives  7.01 us (4%)
  other arithmetic  5.73 us (3%)
  matrix products  2.38 us (1%)
  Pallas kernels  2.23 us (1%)
    reduce_scatter x1, waiting for transfers between devices, local(): summed = lax.psum_scatter(partial, 'z_hi', scatter_dimension=0, tiled=True)  45.8 us
    all_to_all x7, waiting for transfers between devices, exchanged(): return lax.all_to_all(pieces, axes, split_axis=0, concat_axis=0, tiled=True)  39 us
    all_to_all x7, starting transfers between devices, exchanged(): return lax.all_to_all(pieces, axes, split_axis=0, concat_axis=0, tiled=True)  38.9 us
    ppermute x1, starting transfers between devices, local(): other_half = lax.ppermute(own_half, 'core', [(0, 1), (1, 0)])  8.77 us
    all_to_all x1, blocking collectives, exchanged(): return lax.all_to_all(pieces, axes, split_axis=0, concat_axis=0, tiled=True)  7.01 us
    unnamed x15, local copies, waits for them, and re-layouts  3.92 us
  transfers between devices with their start and end apart: 10, of which 7 were waited for; matrix products, arithmetic and copies ran while one was open for 10% of the time, Pallas kernels for 0%

profile of v8, /device:TPU:1, one launch (start us, length us, event | category | flops | bytes accessed | tf_op | source)
XLA Modules:
  0.0 182.1 jit_solution(6894105290988387806)
XLA Ops:
  7.2 1.2 copy.55
  9.7 4.7 %all-to-all-start = ((bf16[4,256,512]{2,1,0:T(8,128)(2,1)}), bf16[4,256,512]{2,1,0:T(8,128)(2,1)S(1)}, u32[]{:S(2)}, u32[]{:S(2)}) async-start(bf16[4,256,512]{2,1,0:T(8,128)(2,1)} %broadcast_in_dim.9), calls=%async_computation | async-start | bytes 2097152 | tf_op jit(solution)/shard_map/all_to_all | solution.py:26
  14.4 1.3 copy.58
  15.6 7.0 %all-to-all-done = bf16[4,256,512]{2,1,0:T(8,128)(2,1)S(1)} async-done(((bf16[4,256,512]{2,1,0:T(8,128)(2,1)}), bf16[4,256,512]{2,1,0:T(8,128)(2,1)S(1)}, u32[]{:S(2)}, u32[]{:S(2)}) %all-to-all-start) | async-done | bytes 1048608 | tf_op jit(solution)/shard_map/all_to_all | solution.py:26
  22.6 3.5 %all-to-all-start.1 = ((bf16[4,256,448]{1,2,0:T(8,128)(2,1)}), bf16[4,256,448]{1,2,0:T(8,128)(2,1)S(1)}, u32[]{:S(2)}, u32[]{:S(2)}) async-start(bf16[4,256,448]{1,2,0:T(8,128)(2,1)} %bitcast.5), calls=%async_computation.1 | async-start | bytes 1835008 | tf_op jit(solution)/shard_map/all_to_all | solution.py:26
  26.2 8.8 %collective-permute-start = (bf16[1024,512]{1,0:T(8,128)(2,1)S(1)}, bf16[1024,512]{1,0:T(8,128)(2,1)}, u32[]{:S(2)}, u32[]{:S(2)}) collective-permute-start(bf16[1024,512]{1,0:T(8,128)(2,1)S(1)} %bitcast.57), channel_id=1, source_target_pairs={{0,1},{1,0},{2,3},{3,2},{4,5},{5,4},{6,7},{7,6},{8,9},{9,8},{10,11... | collective-permute-start | bytes 3145736 | tf_op jit(solution)/shard_map/ppermute | solution.py:109
  35.5 1.9 %collective-permute-done = bf16[1024,512]{1,0:T(8,128)(2,1)} collective-permute-done((bf16[1024,512]{1,0:T(8,128)(2,1)S(1)}, bf16[1024,512]{1,0:T(8,128)(2,1)}, u32[]{:S(2)}, u32[]{:S(2)}) %collective-permute-start) | collective-permute-done | bytes 1048608 | tf_op jit(solution)/shard_map/ppermute | solution.py:109
  37.4 1.5 copy.60
  38.9 2.2 %shard_map.67 = bf16[8,128,448]{2,1,0:T(8,128)(2,1)} custom-call(bf16[4,512,256]{2,1,0:T(8,128)(2,1)S(1)} %bitcast.54, bf16[4,512,256]{2,1,0:T(8,128)(2,1)S(1)} %bitcast.55, bf16[4,448,256]{2,1,0:T(8,128)(2,1)S(1)} %bitcast.56), custom_call_target="tpu_custom_call" | custom-call | flops 939524096 | bytes 3932160 | tf_op jit(solution)/shard_map/pallas_call | solution.py:71
  43.7 3.8 %all-to-all-start.2 = ((f32[4,64,448]{2,1,0:T(8,128)}), f32[4,64,448]{2,1,0:T(8,128)S(1)}, u32[]{:S(2)}, u32[]{:S(2)}) async-start(f32[4,64,448]{2,1,0:T(8,128)} %copy.64), calls=%async_computation.3 | async-start | bytes 1048576 | tf_op jit(solution)/shard_map/all_to_all | solution.py:26
  48.0 1.5 copy.62
  49.9 3.1 %all-to-all-done.2 = f32[4,64,448]{2,1,0:T(8,128)S(1)} async-done(((f32[4,64,448]{2,1,0:T(8,128)}), f32[4,64,448]{2,1,0:T(8,128)S(1)}, u32[]{:S(2)}, u32[]{:S(2)}) %all-to-all-start.2) | async-done | bytes 458784 | tf_op jit(solution)/shard_map/all_to_all | solution.py:26
  53.1 45.8 %reduce-scatter.2.cloned.1.call-done = bf16[1,128,448]{2,1,0:T(8,128)(2,1)} async-done(((bf16[8,128,448]{2,1,0:T(8,128)(2,1)}), bf16[1,128,448]{2,1,0:T(8,128)(2,1)}) %reduce-scatter.2.cloned.1.call-update) | async-done | bytes 114704 | tf_op jit(solution)/shard_map/reduce_scatter | solution.py:115
  100.7 1.7 fusion.17
  103.1 7.0 %all_to_all.40 = f32[4,8,128]{2,1,0:T(8,128)S(1)} all-to-all(f32[4,8,128]{2,1,0:T(8,128)S(1)} %broadcast_in_dim_broadcast_in_dim.3), channel_id=1, replica_groups=mesh['x_lo'=2,'z_hi'=8,'z_lo'=2,'y'=4,'x_hi'=2,'core'=2] {'x_lo','z_lo'}, dimensions={0} | all-to-all | bytes 32768 | tf_op jit(solution)/shard_map/all_to_all | solution.py:26
  110.7 6.2 %all-to-all-start.4 = ((f32[8,8,128]{2,1,0:T(8,128)}), f32[8,8,128]{2,1,0:T(8,128)S(1)}, u32[]{:S(2)}, u32[]{:S(2)}) async-start(f32[8,8,128]{2,1,0:T(8,128)} %broadcast_in_dim.10), calls=%async_computation.5 | async-start | bytes 65536 | tf_op jit(solution)/shard_map/all_to_all | solution.py:26
  117.0 11.9 %all-to-all-done.4 = f32[8,8,128]{2,1,0:T(8,128)S(1)} async-done(((f32[8,8,128]{2,1,0:T(8,128)}), f32[8,8,128]{2,1,0:T(8,128)S(1)}, u32[]{:S(2)}, u32[]{:S(2)}) %all-to-all-start.4) | async-done | bytes 32800 | tf_op jit(solution)/shard_map/all_to_all | solution.py:26
  129.5 13.8 %all-to-all-start.5 = ((f32[16,8,128]{2,1,0:T(8,128)}), f32[16,8,128]{2,1,0:T(8,128)S(1)}, u32[]{:S(2)}, u32[]{:S(2)}) async-start(f32[16,8,128]{2,1,0:T(8,128)} %broadcast_in_dim.11), calls=%async_computation.6 | async-start | bytes 131072 | tf_op jit(solution)/shard_map/all_to_all | solution.py:26
  144.0 6.6 %all-to-all-done.5 = f32[16,8,128]{2,1,0:T(8,128)S(1)} async-done(((f32[16,8,128]{2,1,0:T(8,128)}), f32[16,8,128]{2,1,0:T(8,128)S(1)}, u32[]{:S(2)}, u32[]{:S(2)}) %all-to-all-start.5) | async-done | bytes 65568 | tf_op jit(solution)/shard_map/all_to_all | solution.py:26
  150.6 3.3 %all-to-all-start.7 = ((bf16[4,32,448]{2,1,0:T(8,128)(2,1)}), bf16[4,32,448]{2,1,0:T(8,128)(2,1)S(1)}, u32[]{:S(2)}, u32[]{:S(2)}) async-start(bf16[4,32,448]{2,1,0:T(8,128)(2,1)} %bitcast.29), calls=%async_computation.8 | async-start | bytes 262144 | tf_op jit(solution)/shard_map/all_to_all | solution.py:26
  155.2 2.4 %multiply_convert_fusion = bf16[1024,448]{0,1:T(8,128)(2,1)S(1)} fusion(bf16[1024,1024]{0,1:T(8,128)(2,1)S(1)} %bitcast.64, bf16[1024,512]{1,0:T(8,128)(2,1)} %all-gather.2.cloned.1.call-done, f32[]{:T(128)} %bitcast.24), kind=kOutput, calls=%fused_computation.1 | convolution fusion | flops 940441600 | bytes 4063236 | tf_op jit(solution)/shard_map/dot_general | solution.py:141
  158.6 3.6 %all-to-all-start.6 = ((bf16[4,256,448]{1,2,0:T(8,128)(2,1)}), bf16[4,256,448]{1,2,0:T(8,128)(2,1)S(1)}, u32[]{:S(2)}, u32[]{:S(2)}) async-start(bf16[4,256,448]{1,2,0:T(8,128)(2,1)} %bitcast.53), calls=%async_computation.7 | async-start | bytes 1835008 | tf_op jit(solution)/shard_map/all_to_all | solution.py:26
  163.5 10.5 %all-to-all-done.6 = bf16[4,256,448]{1,2,0:T(8,128)(2,1)S(1)} async-done(((bf16[4,256,448]{1,2,0:T(8,128)(2,1)}), bf16[4,256,448]{1,2,0:T(8,128)(2,1)S(1)}, u32[]{:S(2)}, u32[]{:S(2)}) %all-to-all-start.6) | async-done | bytes 917536 | tf_op jit(solution)/shard_map/all_to_all | solution.py:26
  173.9 1.4 copy.70
  (48 shorter events, 12.6 us)
Async XLA Ops:
  8.5 5.9 %copy-start.3 = (bf16[256,1792]{1,0:T(8,128)(2,1)S(1)}, bf16[256,1792]{1,0:T(8,128)(2,1)}, u32[]{:S(2)}) copy-start(bf16[256,1792]{1,0:T(8,128)(2,1)} %param.4) | copy-start | bytes 2752516
  9.7 12.9 %all-to-all-start = ((bf16[4,256,512]{2,1,0:T(8,128)(2,1)}), bf16[4,256,512]{2,1,0:T(8,128)(2,1)S(1)}, u32[]{:S(2)}, u32[]{:S(2)}) async-start(bf16[4,256,512]{2,1,0:T(8,128)(2,1)} %broadcast_in_dim.9), calls=%async_computation | async-start | bytes 2097152 | tf_op jit(solution)/shard_map/all_to_all | solution.py:26
  22.6 14.7 %copy-start = (bf16[4,256,512]{2,1,0:T(8,128)(2,1)}, bf16[4,256,512]{2,1,0:T(8,128)(2,1)S(1)}, u32[]{:S(2)}) copy-start(bf16[4,256,512]{2,1,0:T(8,128)(2,1)S(1)} %all-to-all-done) | copy-start | bytes 3145732
  22.6 16.2 %all-to-all-start.1 = ((bf16[4,256,448]{1,2,0:T(8,128)(2,1)}), bf16[4,256,448]{1,2,0:T(8,128)(2,1)S(1)}, u32[]{:S(2)}, u32[]{:S(2)}) async-start(bf16[4,256,448]{1,2,0:T(8,128)(2,1)} %bitcast.5), calls=%async_computation.1 | async-start | bytes 1835008 | tf_op jit(solution)/shard_map/all_to_all | solution.py:26
  26.2 72.7 %reduce-scatter.2.cloned.1.call-start = ((), (), s32[]{:S(2)}) async-start(), calls=%async_computation.9 | async-start | bytes 1179648 | tf_op jit(solution)/shard_map/reduce_scatter | solution.py:115
  26.2 11.2 %collective-permute-start = (bf16[1024,512]{1,0:T(8,128)(2,1)S(1)}, bf16[1024,512]{1,0:T(8,128)(2,1)}, u32[]{:S(2)}, u32[]{:S(2)}) collective-permute-start(bf16[1024,512]{1,0:T(8,128)(2,1)S(1)} %bitcast.57), channel_id=1, source_target_pairs={{0,1},{1,0},{2,3},{3,2},{4,5},{5,4},{6,7},{7,6},{8,9},{9,8},{10,11... | collective-permute-start | bytes 3145736 | tf_op jit(solution)/shard_map/ppermute | solution.py:109
  38.9 2.3 %copy-start.4 = (f32[32,1792]{1,0:T(8,128)S(1)}, f32[32,1792]{1,0:T(8,128)}, u32[]{:S(2)}) copy-start(f32[32,1792]{1,0:T(8,128)} %param.7) | copy-start | bytes 688132
  41.2 6.3 %copy-start.1 = (bf16[4,256,512]{2,1,0:T(8,128)(2,1)S(1)}, bf16[4,256,512]{2,1,0:T(8,128)(2,1)}, u32[]{:S(2)}) copy-start(bf16[4,256,512]{2,1,0:T(8,128)(2,1)} %copy-done) | copy-start | bytes 3145732
  43.7 9.3 %all-to-all-start.2 = ((f32[4,64,448]{2,1,0:T(8,128)}), f32[4,64,448]{2,1,0:T(8,128)S(1)}, u32[]{:S(2)}, u32[]{:S(2)}) async-start(f32[4,64,448]{2,1,0:T(8,128)} %copy.64), calls=%async_computation.3 | async-start | bytes 1048576 | tf_op jit(solution)/shard_map/all_to_all | solution.py:26
  47.5 107.7 %all-gather.2.cloned.1.call-start = ((), (), s32[]{:S(2)}) async-start(), calls=%async_computation.10 | async-start | bytes 1179648 | tf_op jit(solution)/shard_map/all_gather | solution.py:130
  98.9 18.1 %copy-start.2 = (bf16[1,128,448]{2,1,0:T(8,128)(2,1)S(1)}, bf16[1,128,448]{2,1,0:T(8,128)(2,1)}, u32[]{:S(2)}) copy-start(bf16[1,128,448]{2,1,0:T(8,128)(2,1)} %reduce-scatter.2.cloned.1.call-done) | copy-start | bytes 344068
  110.7 18.1 %all-to-all-start.4 = ((f32[8,8,128]{2,1,0:T(8,128)}), f32[8,8,128]{2,1,0:T(8,128)S(1)}, u32[]{:S(2)}, u32[]{:S(2)}) async-start(f32[8,8,128]{2,1,0:T(8,128)} %broadcast_in_dim.10), calls=%async_computation.5 | async-start | bytes 65536 | tf_op jit(solution)/shard_map/all_to_all | solution.py:26
  129.5 21.1 %all-to-all-start.5 = ((f32[16,8,128]{2,1,0:T(8,128)}), f32[16,8,128]{2,1,0:T(8,128)S(1)}, u32[]{:S(2)}, u32[]{:S(2)}) async-start(f32[16,8,128]{2,1,0:T(8,128)} %broadcast_in_dim.11), calls=%async_computation.6 | async-start | bytes 131072 | tf_op jit(solution)/shard_map/all_to_all | solution.py:26
  150.6 8.0 %all-to-all-start.7 = ((bf16[4,32,448]{2,1,0:T(8,128)(2,1)}), bf16[4,32,448]{2,1,0:T(8,128)(2,1)S(1)}, u32[]{:S(2)}, u32[]{:S(2)}) async-start(bf16[4,32,448]{2,1,0:T(8,128)(2,1)} %bitcast.29), calls=%async_computation.8 | async-start | bytes 262144 | tf_op jit(solution)/shard_map/all_to_all | solution.py:26
  157.6 5.0 %copy-start.5 = (f32[32,1792]{1,0:T(8,128)S(1)}, f32[32,1792]{1,0:T(8,128)}, u32[]{:S(2)}) copy-start(f32[32,1792]{1,0:T(8,128)} %param.6) | copy-start | bytes 688132
  158.6 15.3 %all-to-all-start.6 = ((bf16[4,256,448]{1,2,0:T(8,128)(2,1)}), bf16[4,256,448]{1,2,0:T(8,128)(2,1)S(1)}, u32[]{:S(2)}, u32[]{:S(2)}) async-start(bf16[4,256,448]{1,2,0:T(8,128)(2,1)} %bitcast.53), calls=%async_computation.7 | async-start | bytes 1835008 | tf_op jit(solution)/shard_map/all_to_all | solution.py:26
Sparse Core Ops, SparseCore 0:
  41.3 57.5 reduce-scatter.1
  101.5 51.2 all-gather.1
